TPU v7x, 512 devices: a whole 4x4x16 slice. The times are simulated.
512 devices in a mesh: wide: 32 (over x, y, core), narrow: 16 (over z).
Axes of the slice: x: 4, y: 4, z: 16, core: 2. Of those that a mesh axis runs over, the one named last changes fastest.
Arguments:
- samples: float32 [256, 65536], P('narrow', 'wide'), may hold values from -6 to 6
- row_weights: float32 [32768], P('narrow'), may hold values from 0.1 to 10
- tile_ranks: int32 [64, 128], P('narrow', 'wide'), may hold values from 16 to 80, as said below
- u_factors: bfloat16 [64, 128, 80, 512], P('narrow', 'wide'), may hold values from -0.078125 to 0.078125
- v_factors: bfloat16 [64, 128, 80, 512], P('narrow', 'wide'), may hold values from -0.25 to 0.25
Outputs:
- forward_rows: float32 [256, 32768], P('wide', 'narrow')
- adjoint_cols: float32 [256, 65536], P(None, ('wide', 'narrow'))
Inputs may be any that keep to these rules, and one draw needn't show every extreme that they name: `tile_ranks`: every rank is a multiple of 16.
All inputs are finite; a program needn't handle non-finite values.
Results may differ from a plain program's by a relative error of at most 0.0085.
Values may be sent and summed in bfloat16 or wider, within the bound.
No kernel may reach another device: no remote copies, remote signals or barrier semaphores. Data moves between devices by JAX's collectives and lax.ppermute only.
A program may use at most 64 MiB of HBM per device.

v0:
```python
import jax
import jax.numpy as jnp
from jax import lax
from jax.sharding import PartitionSpec as P


def copy_for_each(x, axis):
    copies = jnp.broadcast_to(x, (lax.axis_size(axis), *x.shape))
    return lax.all_to_all(copies, axis, split_axis=0, concat_axis=0, tiled=True)


def joined_along(blocks, dim):
    shape = list(blocks.shape[1:])
    shape[dim] *= blocks.shape[0]
    return jnp.moveaxis(blocks, 0, dim).reshape(shape)


def gathered_copies(x, axis, dim):
    blocks = copy_for_each(x, axis)
    return joined_along(blocks, dim)


def cut_along(x, dim, peers):
    before, after = (x.shape[:dim], x.shape[dim + 1 :])
    return jnp.moveaxis(x.reshape(*before, peers, -1, *after), dim, 0)


def sum_at_owner(x, axis, dim):
    peers = lax.axis_size(axis)
    blocks = lax.all_to_all(cut_along(x, dim, peers), axis, 0, 0, tiled=True)
    return jnp.sum(blocks.astype(jnp.float32), axis=0)


def on_device(samples, row_weights, tile_ranks, u_factors, v_factors):
    tile_rows, tile_cols, rank_cap, tile_size = v_factors.shape
    columns = gathered_copies(samples.astype(jnp.bfloat16), "narrow", 0)
    col_count = columns.shape[0]
    columns = columns.reshape(col_count, tile_cols, tile_size)
    levels = lax.broadcasted_iota(jnp.int32, (1, 1, rank_cap), 2)
    rank_mask = (levels < tile_ranks[:, :, None]).astype(jnp.float32)[:, :, :, None]
    coeffs = jnp.einsum("sjb,ijrb->ijrs", columns, v_factors, preferred_element_type=jnp.float32)
    coeffs = (coeffs * rank_mask).astype(jnp.bfloat16)
    partial_value = jnp.einsum(
        "ijrs,ijrb->sib", coeffs, u_factors, preferred_element_type=jnp.float32
    )
    partial_value = partial_value.reshape(col_count, tile_rows * tile_size)
    forward_rows = sum_at_owner(partial_value.astype(jnp.bfloat16), "wide", 0)
    weighted_share = (forward_rows * row_weights[None, :]).astype(jnp.bfloat16)
    weighted = gathered_copies(weighted_share, "wide", 0)
    weighted = weighted.reshape(col_count, tile_rows, tile_size)
    adjoint_coeffs = jnp.einsum(
        "sib,ijrb->ijrs", weighted, u_factors, preferred_element_type=jnp.float32
    )
    adjoint_coeffs = (adjoint_coeffs * rank_mask).astype(jnp.bfloat16)
    back = jnp.einsum(
        "ijrs,ijrb->sjb", adjoint_coeffs, v_factors, preferred_element_type=jnp.float32
    )
    back = back.reshape(col_count, tile_cols * tile_size)
    adjoint_cols = sum_at_owner(back.astype(jnp.bfloat16), "narrow", 1)
    return (forward_rows, adjoint_cols)


def solution(mesh):
    in_specs = (
        P("narrow", "wide"),
        P("narrow"),
        P("narrow", "wide"),
        P("narrow", "wide", None, None),
        P("narrow", "wide", None, None),
    )
    out_specs = (P("wide", "narrow"), P(None, ("wide", "narrow")))
    return jax.shard_map(
        on_device, mesh=mesh, in_specs=in_specs, out_specs=out_specs, check_vma=False
    )
```

profile of v0, /device:TPU:32, one launch (start us, length us, event | category | flops | bytes accessed | tf_op | source)
XLA Modules:
  0.0 188.3 jit_solution(6365505221175190505)
XLA Ops:
  0.6 0.0 copy-start
  0.6 1.0 convert_element_type.48
  1.7 1.1 broadcast_in_dim.4
  2.8 15.3 %all-to-all-start = ((bf16[16,16,2048]{2,1,0:T(8,128)(2,1)}), bf16[16,16,2048]{2,1,0:T(8,128)(2,1)S(1)}, u32[]{:S(2)}, u32[]{:S(2)}) async-start(bf16[16,16,2048]{2,1,0:T(8,128)(2,1)} %broadcast_in_dim.4), calls=%async_computation | async-start | bytes 2097152 | tf_op jit(solution)/shard_map/all_to_all | solution.py:9
  18.1 0.1 fusion.22
  18.2 49.2 %all-to-all-done = bf16[16,16,2048]{2,1,0:T(8,128)(2,1)S(1)} async-done(((bf16[16,16,2048]{2,1,0:T(8,128)(2,1)}), bf16[16,16,2048]{2,1,0:T(8,128)(2,1)S(1)}, u32[]{:S(2)}, u32[]{:S(2)}) %all-to-all-start) | async-done | bytes 1048608 | tf_op jit(solution)/shard_map/all_to_all | solution.py:9
  67.4 0.8 reshape_reshape.6
  68.2 3.7 %fusion.1 = bf16[256,4,512]{2,0,1:T(8,128)(2,1)} fusion(bf16[4,4,80,512]{3,2,1,0:T(8,128)(2,1)S(1)} %copy-done, bf16[4,4,80,512]{3,2,1,0:T(8,128)(2,1)} %param.9, bf16[256,4,512]{2,1,0:T(4,128)(2,1)S(1)} %reshape_reshape.6, f32[4,4,80]{2,1,0:T(4,128)S(1)} %fusion.22), kind=kOutput, calls=%fused_computation.7 | convolution fusion | flops 672268288 | bytes 4723712 | tf_op jit(solution)/shard_map/ijrs,ijrb->sib/dot_general | solution.py:43
  71.8 2.0 %copy.22 = bf16[256,4,512]{2,1,0:T(4,128)(2,1)S(1)} copy(bf16[256,4,512]{2,0,1:T(8,128)(2,1)} %fusion.1) | data formatting | bytes 2097152 | tf_op jit(solution)/shard_map/convert_element_type | solution.py:47
  73.9 0.8 convert_element_type.53
  74.7 0.0 copy-start.2
  74.7 23.9 %all_to_all.20 = bf16[32,8,2048]{2,1,0:T(8,128)(2,1)S(1)} all-to-all(bf16[32,8,2048]{2,1,0:T(8,128)(2,1)S(1)} %convert_element_type.53), channel_id=1, replica_groups=mesh['wide'=32,'narrow'=16] {'wide'}, dimensions={0} | all-to-all | bytes 2097152 | tf_op jit(solution)/shard_map/all_to_all | solution.py:30
  98.6 0.2 convert_reduce_fusion.1
  98.8 0.0 copy-done.2
  98.8 0.0 copy-start.1
  98.8 1.1 broadcast_in_dim.10
  99.9 4.0 %all-to-all-start.2 = ((bf16[32,8,2048]{2,1,0:T(8,128)(2,1)}), bf16[32,8,2048]{2,1,0:T(8,128)(2,1)S(1)}, u32[]{:S(2)}, u32[]{:S(2)}) async-start(bf16[32,8,2048]{2,1,0:T(8,128)(2,1)} %broadcast_in_dim.10), calls=%async_computation.2 | async-start | bytes 2097152 | tf_op jit(solution)/shard_map/all_to_all | solution.py:9
  104.0 16.8 %all-to-all-done.2 = bf16[32,8,2048]{2,1,0:T(8,128)(2,1)S(1)} async-done(((bf16[32,8,2048]{2,1,0:T(8,128)(2,1)}), bf16[32,8,2048]{2,1,0:T(8,128)(2,1)S(1)}, u32[]{:S(2)}, u32[]{:S(2)}) %all-to-all-start.2) | async-done | bytes 1048608 | tf_op jit(solution)/shard_map/all_to_all | solution.py:9
  120.7 0.8 reshape_reshape.7
  121.5 3.7 %fusion.2 = bf16[256,4,512]{2,0,1:T(8,128)(2,1)} fusion(bf16[4,4,80,512]{3,2,1,0:T(8,128)(2,1)} %param.9, bf16[4,4,80,512]{3,2,1,0:T(8,128)(2,1)S(1)} %copy-done, bf16[256,4,512]{2,1,0:T(4,128)(2,1)S(1)} %reshape_reshape.7, f32[4,4,80]{2,0,1:T(4,128)S(1)} %copy.25), kind=kOutput, calls=%fused_computation.8 | convolution fusion | flops 672268288 | bytes 4723712 | tf_op jit(solution)/shard_map/ijrs,ijrb->sjb/dot_general | solution.py:55
  125.2 1.5 copy.27
  126.7 60.7 %all_to_all.21 = bf16[16,256,128]{1,2,0:T(8,128)(2,1)S(1)} all-to-all(bf16[16,256,128]{1,2,0:T(8,128)(2,1)S(1)} %bitcast.39), channel_id=1, replica_groups=mesh['wide'=32,'narrow'=16] {'narrow'}, dimensions={0} | all-to-all | bytes 2097152 | tf_op jit(solution)/shard_map/all_to_all | solution.py:30
  187.4 0.1 convert_reduce_fusion
  187.5 0.8 copy.28
  (6 shorter events, 0.0 us)
Async XLA Ops:
  0.6 67.6 %copy-start = (bf16[4,4,80,512]{3,2,1,0:T(8,128)(2,1)S(1)}, bf16[4,4,80,512]{3,2,1,0:T(8,128)(2,1)}, u32[]{:S(2)}) copy-start(bf16[4,4,80,512]{3,2,1,0:T(8,128)(2,1)} %param.8) | copy-start | bytes 3932164
  2.8 15.3 %copy-start.3 = (s32[4,4]{1,0:T(4,128)S(1)}, s32[4,4]{1,0:T(4,128)}, u32[]{:S(2)}) copy-start(s32[4,4]{1,0:T(4,128)} %param.7) | copy-start | bytes 196
  2.8 64.6 %all-to-all-start = ((bf16[16,16,2048]{2,1,0:T(8,128)(2,1)}), bf16[16,16,2048]{2,1,0:T(8,128)(2,1)S(1)}, u32[]{:S(2)}, u32[]{:S(2)}) async-start(bf16[16,16,2048]{2,1,0:T(8,128)(2,1)} %broadcast_in_dim.4), calls=%async_computation | async-start | bytes 2097152 | tf_op jit(solution)/shard_map/all_to_all | solution.py:9
  74.7 24.1 %copy-start.2 = (f32[2048]{0:T(1024)S(1)}, f32[2048]{0:T(1024)}, u32[]{:S(2)}) copy-start(f32[2048]{0:T(1024)} %param.6) | copy-start | bytes 24580
  98.8 1.1 copy-start.1
  99.9 20.8 %all-to-all-start.2 = ((bf16[32,8,2048]{2,1,0:T(8,128)(2,1)}), bf16[32,8,2048]{2,1,0:T(8,128)(2,1)S(1)}, u32[]{:S(2)}, u32[]{:S(2)}) async-start(bf16[32,8,2048]{2,1,0:T(8,128)(2,1)} %broadcast_in_dim.10), calls=%async_computation.2 | async-start | bytes 2097152 | tf_op jit(solution)/shard_map/all_to_all | solution.py:9
where the time goes:
time: 189 us; the launch traced here: 188 us
  blocking collectives  84.6 us (45%)
  waiting for transfers between devices  66 us (35%)
  starting transfers between devices  19.4 us (10%)
  local copies, waits for them, and re-layouts  8.85 us (5%)
  matrix products  7.32 us (4%)
    all_to_all x2, blocking collectives, sum_at_owner(): blocks = lax.all_to_all(cut_along(x, dim, peers), axis, 0, 0, tiled=True)  84.6 us
    all_to_all x2, waiting for transfers between devices, copy_for_each(): return lax.all_to_all(copies, axis, split_axis=0, concat_axis=0, tiled=True)  66 us
    all_to_all x2, starting transfers between devices, copy_for_each(): return lax.all_to_all(copies, axis, split_axis=0, concat_axis=0, tiled=True)  19.4 us
  transfers between devices with their start and end apart: 2, of which 2 were waited for; matrix products, arithmetic and copies ran while one was open for 0% of the time, Pallas kernels for 0%

commit v1 on v0

v1 whole, which is shorter than its diff:
```python
import functools

import jax
import jax.numpy as jnp
from jax import lax
from jax.experimental import pallas as pl
from jax.experimental.pallas import tpu as pltpu
from jax.sharding import Mesh
from jax.sharding import PartitionSpec as P

LINE = ("zh", "zl")
PAIR_LINE = ("c", "zh", "zl")
NT = (((1,), (1,)), ((), ()))
TN = (((0,), (0,)), ((), ()))


def turned(steps):
    return [
        (c * 16 + z, c * 16 + (z + (steps if c == 0 else -steps)) % 16)
        for c in range(2)
        for z in range(16)
    ]


def forward_kernel(at, own, one, two, low, high, v0, v1, u0, u1, out, coeffs):
    core = at[0]
    for k, v in enumerate((v0, v1)):
        side = jnp.bitwise_xor(core, k)
        for j in range(4):
            cols = pl.ds(j * 512, 512)
            x = jnp.concatenate([piece[side, :, cols] for piece in (own, one, two, low, high)], 0)
            tall = jnp.concatenate([v[i, j] for i in range(4)], 0)
            c = lax.dot_general(tall, x, NT, preferred_element_type=jnp.float32)
            for i in range(4):
                coeffs[i, pl.ds(k * 320 + j * 80, 80), :] = c[i * 80 : i * 80 + 80].astype(jnp.bfloat16)
    for i in range(4):
        u = jnp.concatenate([u[i, j] for u in (u0, u1) for j in range(4)], 0)
        part = lax.dot_general(coeffs[i], u, TN, preferred_element_type=jnp.float32)
        for p in range(4):
            for zh in range(4):
                row = p * 32 + zh * 8
                out[zh * 4 + at[1 + p], :, pl.ds(i * 512, 512)] = part[row : row + 8].astype(jnp.bfloat16)


def adjoint_kernel(at, w, v0, v1, u0, u1, own, one, two, low, high, coeffs, blocks):
    core = at[0]
    for k, u in enumerate((u0, u1)):
        for i in range(4):
            tall = jnp.concatenate([u[i, j] for j in range(4)], 0)
            a = lax.dot_general(tall, w[:, pl.ds(i * 512, 512)], NT, preferred_element_type=jnp.float32)
            for j in range(4):
                coeffs[k, j, pl.ds(i * 80, 80), :] = a[j * 80 : j * 80 + 80].astype(jnp.bfloat16)
    for k, v in enumerate((v0, v1)):
        side = jnp.bitwise_xor(core, k)
        for j in range(4):
            tall = jnp.concatenate([v[i, j] for i in range(4)], 0)
            back = lax.dot_general(coeffs[k, j], tall, TN, preferred_element_type=jnp.float32)
            back = back.astype(jnp.bfloat16)
            for q in range(4):
                blocks[q, side, j] = back[:, q * 128 : q * 128 + 128]
    own[...] = blocks[at[1]]
    one[...] = blocks[at[2]]
    two[...] = blocks[at[3]]
    low[...] = blocks[at[4], :, :2]
    high[...] = blocks[at[4], :, 2:]


SMEM = pl.BlockSpec(memory_space=pltpu.SMEM)
VMEM = pl.BlockSpec(memory_space=pltpu.VMEM)


def forward_part(at, pieces, v, u):
    return pl.pallas_call(
        forward_kernel,
        out_shape=jax.ShapeDtypeStruct((16, 8, 2048), jnp.bfloat16),
        in_specs=[SMEM] + [VMEM] * 9,
        out_specs=VMEM,
        scratch_shapes=[pltpu.VMEM((4, 640, 128), jnp.bfloat16)],
        name="forward_part",
    )(at, *pieces, *v, *u)


def adjoint_part(at, weighted, v, u):
    full = jax.ShapeDtypeStruct((2, 4, 128, 128), jnp.bfloat16)
    half = jax.ShapeDtypeStruct((2, 2, 128, 128), jnp.bfloat16)
    return pl.pallas_call(
        adjoint_kernel,
        out_shape=(full, full, full, half, half),
        in_specs=[SMEM] + [VMEM] * 5,
        out_specs=(VMEM,) * 5,
        scratch_shapes=[
            pltpu.VMEM((2, 4, 320, 128), jnp.bfloat16),
            pltpu.VMEM((4, 2, 4, 128, 128), jnp.bfloat16),
        ],
        name="adjoint_part",
    )(at, weighted, *v, *u)


def exchange(blocks, axes):
    return lax.all_to_all(blocks, axes, split_axis=0, concat_axis=0, tiled=True)


def to_neighbours(own, one, two, low, high):
    del own
    got_one = lax.ppermute(one, PAIR_LINE, turned(1))
    got_two = lax.ppermute(two, PAIR_LINE, turned(-1))
    got_low = lax.ppermute(low, PAIR_LINE, turned(2))
    got_high = lax.ppermute(high, PAIR_LINE, turned(-2))
    return got_one, got_two, got_low, got_high


def on_device(samples, row_weights, tile_ranks, u_factors, v_factors):
    core = lax.axis_index("c")
    place = lax.axis_index("zl")
    turn = 1 - 2 * core
    swap = functools.partial(lax.ppermute, axis_name="c", perm=[(0, 1), (1, 0)])

    x = samples.astype(jnp.bfloat16).reshape(2, 1, 8, 2048)
    x = jnp.broadcast_to(x, (2, 4, 8, 2048)).reshape(8, 8, 2048)
    far = exchange(x, ("c", "zh")).reshape(2, 32, 2048)
    v = (v_factors, swap(v_factors))
    levels = lax.broadcasted_iota(jnp.int32, (1, 1, 80, 1), 2)
    kept = jnp.where(levels < tile_ranks[:, :, None, None], u_factors, jnp.zeros_like(u_factors))
    u = (kept, swap(kept))

    one, two, low, high = to_neighbours(far, far, far, far[:, :16], far[:, 16:])
    at = jnp.stack([core, place, (place - turn) % 4, (place + turn) % 4, (place + 2) % 4]).astype(jnp.int32)
    part = forward_part(at, (far, one, two, low, high), v, u)
    forward_rows = jnp.sum(exchange(part, ("xy",)).astype(jnp.float32), axis=0)

    weighted = (forward_rows * row_weights[None, :]).astype(jnp.bfloat16)
    weighted = exchange(jnp.broadcast_to(weighted, (16, 8, 2048)), ("xy",)).reshape(128, 2048)

    to = jnp.stack([core, place, (place + turn) % 4, (place - turn) % 4, (place + 2) % 4]).astype(jnp.int32)
    blocks = adjoint_part(to, weighted, v, u)
    one, two, low, high = to_neighbours(*blocks)
    wide = lambda b: b.astype(jnp.float32)
    near = wide(blocks[0]) + wide(one) + wide(two) + wide(jnp.concatenate([low, high], 1))
    near = near.astype(jnp.bfloat16).reshape(8, 128, 128)
    back = exchange(near, ("c", "zh")).reshape(2, 4, 16, 8, 128)
    back = jnp.sum(back.astype(jnp.float32), axis=1)
    adjoint_cols = jnp.swapaxes(back, 0, 1).reshape(256, 128)
    return forward_rows, adjoint_cols


def solution(mesh):
    fine = Mesh(mesh.devices.reshape(16, 2, 4, 4), ("xy", "c", "zh", "zl"))
    narrow, wide = LINE, ("xy", "c")
    in_specs = (
        P(narrow, wide),
        P(narrow),
        P(narrow, wide),
        P(narrow, wide, None, None),
        P(narrow, wide, None, None),
    )
    out_specs = (P(wide, narrow), P(None, (*wide, *narrow)))
    return jax.shard_map(on_device, mesh=fine, in_specs=in_specs, out_specs=out_specs, check_vma=False)
```

time: 189 us -> 149 us (0.79)
  the two profiles are of different devices: /device:TPU:32 before, /device:TPU:1 now
where the time goes in v1:
time: 149 us; the launch traced here: 148 us
  starting transfers between devices  54.7 us (37%)
  blocking collectives  44 us (30%)
  waiting for transfers between devices  27.8 us (19%)
  Pallas kernels  10.1 us (7%)
  local copies, waits for them, and re-layouts  5.75 us (4%)
  other arithmetic  4.54 us (3%)
    all_to_all x2, blocking collectives, exchange(): return lax.all_to_all(blocks, axes, split_axis=0, concat_axis=0, tiled=True)  44 us
    all_to_all x2, starting transfers between devices, exchange(): return lax.all_to_all(blocks, axes, split_axis=0, concat_axis=0, tiled=True)  20.2 us
    all_to_all x2, waiting for transfers between devices, exchange(): return lax.all_to_all(blocks, axes, split_axis=0, concat_axis=0, tiled=True)  18.4 us
    ppermute x2, starting transfers between devices, to_neighbours(): got_high = lax.ppermute(high, PAIR_LINE, turned(-2))  11 us
    ppermute x2, starting transfers between devices, to_neighbours(): got_one = lax.ppermute(one, PAIR_LINE, turned(1))  8.69 us
    ppermute x2, waiting for transfers between devices, to_neighbours(): got_low = lax.ppermute(low, PAIR_LINE, turned(2))  7.22 us
    ppermute x2, starting transfers between devices, to_neighbours(): got_low = lax.ppermute(low, PAIR_LINE, turned(2))  6.69 us
    pallas_call x1, Pallas kernels, adjoint_part(): pl.pallas_call(adjoint_kernel, out_shape=(full, full, full, half, half),...  5.09 us
  transfers between devices with their start and end apart: 12, of which 5 were waited for; matrix products, arithmetic and copies ran while one was open for 3% of the time, Pallas kernels for 0%

profile of v1, /device:TPU:1, one launch (start us, length us, event | category | flops | bytes accessed | tf_op | source)
XLA Modules:
  0.0 147.8 jit_solution(3116574250152857174)
XLA Ops:
  0.6 0.9 convert_bitcast_fusion
  2.3 16.6 %all-to-all-start = ((bf16[8,8,2048]{2,1,0:T(8,128)(2,1)}), bf16[8,8,2048]{2,1,0:T(8,128)(2,1)S(1)}, u32[]{:S(2)}, u32[]{:S(2)}) async-start(bf16[8,8,2048]{2,1,0:T(8,128)(2,1)} %bitcast.6), calls=%async_computation | async-start | bytes 524288 | tf_op jit(solution)/shard_map/all_to_all | solution.py:100
  19.6 1.7 %broadcast_select_fusion.u0 = bf16[4,4,80,512]{3,2,1,0:T(8,128)(2,1)S(1)} fusion(bf16[4,4,80,512]{3,2,1,0:T(8,128)(2,1)} %param.8, pred[4,4,80]{2,1,0:T(4,128)(4,1)S(1)} %iota_compare_fusion), kind=kLoop, calls=%fused_computation | loop fusion | flops 655360 | bytes 2622720 | tf_op jit(solution)/shard_map/jit(_where)/select_n | solution.py:123
  21.3 1.9 %collective-permute-start.5 = (bf16[4,4,80,512]{3,2,1,0:T(8,128)(2,1)S(1)}, bf16[4,4,80,512]{3,2,1,0:T(8,128)(2,1)}, u32[]{:S(2)}, u32[]{:S(2)}) collective-permute-start(bf16[4,4,80,512]{3,2,1,0:T(8,128)(2,1)S(1)} %broadcast_select_fusion.u0), channel_id=1, source_target_pairs={{0,16},{16,0},{1,17},{17,1},{2,18},{18,2},{3,19},{19,3},{4,20},{20... | collective-permute-start | bytes 3932168 | tf_op jit(solution)/shard_map/ppermute | solution.py:124
  23.2 2.4 %collective-permute-start.4 = (bf16[4,4,80,512]{3,2,1,0:T(8,128)(2,1)S(1)}, bf16[4,4,80,512]{3,2,1,0:T(8,128)(2,1)}, u32[]{:S(2)}, u32[]{:S(2)}) collective-permute-start(bf16[4,4,80,512]{3,2,1,0:T(8,128)(2,1)S(1)} %copy-done.1), channel_id=1, source_target_pairs={{0,16},{16,0},{1,17},{17,1},{2,18},{18,2},{3,19},{19,3},{4,20},{20... | collective-permute-start | bytes 3932168 | tf_op jit(solution)/shard_map/ppermute | solution.py:121
  25.6 10.1 %all-to-all-done = bf16[8,8,2048]{2,1,0:T(8,128)(2,1)S(1)} async-done(((bf16[8,8,2048]{2,1,0:T(8,128)(2,1)}), bf16[8,8,2048]{2,1,0:T(8,128)(2,1)S(1)}, u32[]{:S(2)}, u32[]{:S(2)}) %all-to-all-start) | async-done | bytes 262176 | tf_op jit(solution)/shard_map/all_to_all | solution.py:100
  36.4 6.9 %collective-permute-start.3 = (bf16[2,16,2048]{2,1,0:T(8,128)(2,1)S(1)}, bf16[2,16,2048]{2,1,0:T(8,128)(2,1)S(1)}, u32[]{:S(2)}, u32[]{:S(2)}) collective-permute-start(bf16[2,16,2048]{2,1,0:T(8,128)(2,1)S(1)} %get-tuple-element.12), channel_id=1, source_target_pairs={{0,14},{1,15},{2,0},{3,1},{4,2},{5,3},{6,4},{7,5},{8,6},{9,7},{10,... | collective-permute-start | bytes 393224 | tf_op jit(solution)/shard_map/ppermute | solution.py:108
  43.3 1.9 %collective-permute-start.1 = (bf16[2,32,2048]{2,1,0:T(8,128)(2,1)S(1)}, bf16[2,32,2048]{2,1,0:T(8,128)(2,1)S(1)}, u32[]{:S(2)}, u32[]{:S(2)}) collective-permute-start(bf16[2,32,2048]{2,1,0:T(8,128)(2,1)S(1)} %bitcast.16), channel_id=1, source_target_pairs={{0,15},{1,0},{2,1},{3,2},{4,3},{5,4},{6,5},{7,6},{8,7},{9,8},{10,9... | collective-permute-start | bytes 786440 | tf_op jit(solution)/shard_map/ppermute | solution.py:106
  45.2 4.6 %collective-permute-start = (bf16[2,32,2048]{2,1,0:T(8,128)(2,1)S(1)}, bf16[2,32,2048]{2,1,0:T(8,128)(2,1)S(1)}, u32[]{:S(2)}, u32[]{:S(2)}) collective-permute-start(bf16[2,32,2048]{2,1,0:T(8,128)(2,1)S(1)} %bitcast.17), channel_id=1, source_target_pairs={{0,1},{1,2},{2,3},{3,4},{4,5},{5,6},{6,7},{7,8},{8,9},{9,10},{10,1... | collective-permute-start | bytes 786440 | tf_op jit(solution)/shard_map/ppermute | solution.py:105
  49.8 2.7 %collective-permute-start.2 = (bf16[2,16,2048]{2,1,0:T(8,128)(2,1)}, bf16[2,16,2048]{2,1,0:T(8,128)(2,1)}, u32[]{:S(2)}, u32[]{:S(2)}) collective-permute-start(bf16[2,16,2048]{2,1,0:T(8,128)(2,1)} %get-tuple-element.13), channel_id=1, source_target_pairs={{0,2},{1,3},{2,4},{3,5},{4,6},{5,7},{6,8},{7,9},{8,10},{9,11},{10,... | collective-permute-start | bytes 393224 | tf_op jit(solution)/shard_map/ppermute | solution.py:107
  53.2 5.1 %collective-permute-done.2.low = bf16[2,16,2048]{2,1,0:T(8,128)(2,1)} collective-permute-done((bf16[2,16,2048]{2,1,0:T(8,128)(2,1)}, bf16[2,16,2048]{2,1,0:T(8,128)(2,1)}, u32[]{:S(2)}, u32[]{:S(2)}) %collective-permute-start.2) | collective-permute-done | bytes 131104 | tf_op jit(solution)/shard_map/ppermute | solution.py:107
  59.2 5.1 %forward_part.1 = bf16[16,8,2048]{2,1,0:T(8,128)(2,1)} custom-call(s32[5]{0:T(128)} %stack.31.at, bf16[2,32,2048]{2,1,0:T(8,128)(2,1)} %bitcast.18, bf16[2,32,2048]{2,1,0:T(8,128)(2,1)} %copy-done.5, bf16[2,32,2048]{2,1,0:T(8,128)(2,1)} %copy-done.4, bf16[2,16,2048]{2,1,0:T(8,128)(2,1)} %collective-permute-done.2.low, bf16[2,16,2048]{2,1,0:T(8,128)(2,1)} %copy-done.7, ...), custom_call_target="tpu_custom_call" | custom-call | tf_op jit(solution)/shard_map/forward_part/pallas_call | solution.py:73
  64.3 16.1 %all_to_all.20 = bf16[16,8,2048]{2,1,0:T(8,128)(2,1)S(1)} all-to-all(bf16[16,8,2048]{2,1,0:T(8,128)(2,1)} %forward_part.1), channel_id=1, replica_groups=mesh['xy'=16,'c'=2,'zh'=4,'zl'=4] {'xy'}, dimensions={0} | all-to-all | bytes 1048576 | tf_op jit(solution)/shard_map/all_to_all | solution.py:100
  81.4 3.6 %all-to-all-start.2 = ((bf16[16,8,2048]{2,1,0:T(8,128)(2,1)}), bf16[16,8,2048]{2,1,0:T(8,128)(2,1)S(1)}, u32[]{:S(2)}, u32[]{:S(2)}) async-start(bf16[16,8,2048]{2,1,0:T(8,128)(2,1)} %broadcast_in_dim.27), calls=%async_computation.2 | async-start | bytes 1048576 | tf_op jit(solution)/shard_map/all_to_all | solution.py:100
  85.6 8.3 %all-to-all-done.2 = bf16[16,8,2048]{2,1,0:T(8,128)(2,1)S(1)} async-done(((bf16[16,8,2048]{2,1,0:T(8,128)(2,1)}), bf16[16,8,2048]{2,1,0:T(8,128)(2,1)S(1)}, u32[]{:S(2)}, u32[]{:S(2)}) %all-to-all-start.2) | async-done | bytes 524320 | tf_op jit(solution)/shard_map/all_to_all | solution.py:100
  94.7 5.1 %adjoint_part.1 = (bf16[2,4,128,128]{3,2,1,0:T(8,128)(2,1)}, bf16[2,4,128,128]{3,2,1,0:T(8,128)(2,1)}, bf16[2,4,128,128]{3,2,1,0:T(8,128)(2,1)}, bf16[2,2,128,12...) custom-call(s32[5]{0:T(128)} %stack.32.at, bf16[128,2048]{1,0:T(8,128)(2,1)} %bitcast.19, bf16[4,4,80,512]{3,2,1,0:T(8,128)(2,1)} %v0.3, ...), custom_call_target="tpu_custom_call" | custom-call | tf_op jit(solution)/shard_map/adjoint_part/pallas_call | solution.py:86
  99.8 4.1 %collective-permute-start.6 = (bf16[2,4,128,128]{3,2,1,0:T(8,128)(2,1)}, bf16[2,4,128,128]{3,2,1,0:T(8,128)(2,1)S(1)}, u32[]{:S(2)}, u32[]{:S(2)}) collective-permute-start(bf16[2,4,128,128]{3,2,1,0:T(8,128)(2,1)} %get-tuple-element.8), channel_id=1, source_target_pairs={{0,1},{1,2},{2,3},{3,4},{4,5},{5,6},{6,7},{7,8},{8,9},{9,10},{10,1... | collective-permute-start | bytes 786440 | tf_op jit(solution)/shard_map/ppermute | solution.py:105
  103.9 1.9 %collective-permute-start.7 = (bf16[2,4,128,128]{3,2,1,0:T(8,128)(2,1)}, bf16[2,4,128,128]{3,2,1,0:T(8,128)(2,1)S(1)}, u32[]{:S(2)}, u32[]{:S(2)}) collective-permute-start(bf16[2,4,128,128]{3,2,1,0:T(8,128)(2,1)} %get-tuple-element.9), channel_id=1, source_target_pairs={{0,15},{1,0},{2,1},{3,2},{4,3},{5,4},{6,5},{7,6},{8,7},{9,8},{10,9... | collective-permute-start | bytes 786440 | tf_op jit(solution)/shard_map/ppermute | solution.py:106
  105.9 4.0 %collective-permute-start.8 = (bf16[2,2,128,128]{3,2,1,0:T(8,128)(2,1)}, bf16[2,2,128,128]{3,2,1,0:T(8,128)(2,1)S(1)}, u32[]{:S(2)}, u32[]{:S(2)}) collective-permute-start(bf16[2,2,128,128]{3,2,1,0:T(8,128)(2,1)} %get-tuple-element.10), channel_id=1, source_target_pairs={{0,2},{1,3},{2,4},{3,5},{4,6},{5,7},{6,8},{7,9},{8,10},{9,11},{10,... | collective-permute-start | bytes 393224 | tf_op jit(solution)/shard_map/ppermute | solution.py:107
  109.8 4.1 %collective-permute-start.9 = (bf16[2,2,128,128]{3,2,1,0:T(8,128)(2,1)}, bf16[2,2,128,128]{3,2,1,0:T(8,128)(2,1)S(1)}, u32[]{:S(2)}, u32[]{:S(2)}) collective-permute-start(bf16[2,2,128,128]{3,2,1,0:T(8,128)(2,1)} %get-tuple-element.11), channel_id=1, source_target_pairs={{0,14},{1,15},{2,0},{3,1},{4,2},{5,3},{6,4},{7,5},{8,6},{9,7},{10,... | collective-permute-start | bytes 393224 | tf_op jit(solution)/shard_map/ppermute | solution.py:108
  113.9 2.1 %collective-permute-done.8 = bf16[2,2,128,128]{3,2,1,0:T(8,128)(2,1)S(1)} collective-permute-done((bf16[2,2,128,128]{3,2,1,0:T(8,128)(2,1)}, bf16[2,2,128,128]{3,2,1,0:T(8,128)(2,1)S(1)}, u32[]{:S(2)}, u32[]{:S(2)}) %collective-permute-start.8) | collective-permute-done | bytes 131104 | tf_op jit(solution)/shard_map/ppermute | solution.py:107
  116.0 2.1 %collective-permute-done.9 = bf16[2,2,128,128]{3,2,1,0:T(8,128)(2,1)S(1)} collective-permute-done((bf16[2,2,128,128]{3,2,1,0:T(8,128)(2,1)}, bf16[2,2,128,128]{3,2,1,0:T(8,128)(2,1)S(1)}, u32[]{:S(2)}, u32[]{:S(2)}) %collective-permute-start.9) | collective-permute-done | bytes 131104 | tf_op jit(solution)/shard_map/ppermute | solution.py:108
  118.1 1.1 add_convert_fusion
  119.2 27.9 %all_to_all.21 = bf16[8,128,128]{2,1,0:T(8,128)(2,1)S(1)} all-to-all(bf16[8,128,128]{2,1,0:T(8,128)(2,1)S(1)} %bitcast.20), channel_id=1, replica_groups=mesh['xy'=16,'c'=2,'zh'=4,'zl'=4] {'c','zh'}, dimensions={0} | all-to-all | bytes 524288 | tf_op jit(solution)/shard_map/all_to_all | solution.py:100
  (35 shorter events, 6.6 us)
Async XLA Ops:
  2.3 33.4 %all-to-all-start = ((bf16[8,8,2048]{2,1,0:T(8,128)(2,1)}), bf16[8,8,2048]{2,1,0:T(8,128)(2,1)S(1)}, u32[]{:S(2)}, u32[]{:S(2)}) async-start(bf16[8,8,2048]{2,1,0:T(8,128)(2,1)} %bitcast.6), calls=%async_computation | async-start | bytes 524288 | tf_op jit(solution)/shard_map/all_to_all | solution.py:100
  19.6 3.6 %copy-start.1 = (bf16[4,4,80,512]{3,2,1,0:T(8,128)(2,1)S(1)}, bf16[4,4,80,512]{3,2,1,0:T(8,128)(2,1)}, u32[]{:S(2)}) copy-start(bf16[4,4,80,512]{3,2,1,0:T(8,128)(2,1)} %v0.3) | copy-start | bytes 3932164
  21.3 37.2 %copy-start = (bf16[4,4,80,512]{3,2,1,0:T(8,128)(2,1)}, bf16[4,4,80,512]{3,2,1,0:T(8,128)(2,1)S(1)}, u32[]{:S(2)}) copy-start(bf16[4,4,80,512]{3,2,1,0:T(8,128)(2,1)S(1)} %broadcast_select_fusion.u0) | copy-start | bytes 3932164
  21.3 37.1 %collective-permute-start.5 = (bf16[4,4,80,512]{3,2,1,0:T(8,128)(2,1)S(1)}, bf16[4,4,80,512]{3,2,1,0:T(8,128)(2,1)}, u32[]{:S(2)}, u32[]{:S(2)}) collective-permute-start(bf16[4,4,80,512]{3,2,1,0:T(8,128)(2,1)S(1)} %broadcast_select_fusion.u0), channel_id=1, source_target_pairs={{0,16},{16,0},{1,17},{17,1},{2,18},{18,2},{3,19},{19,3},{4,20},{20... | collective-permute-start | bytes 3932168 | tf_op jit(solution)/shard_map/ppermute | solution.py:124
  23.2 35.2 %collective-permute-start.4 = (bf16[4,4,80,512]{3,2,1,0:T(8,128)(2,1)S(1)}, bf16[4,4,80,512]{3,2,1,0:T(8,128)(2,1)}, u32[]{:S(2)}, u32[]{:S(2)}) collective-permute-start(bf16[4,4,80,512]{3,2,1,0:T(8,128)(2,1)S(1)} %copy-done.1), channel_id=1, source_target_pairs={{0,16},{16,0},{1,17},{17,1},{2,18},{18,2},{3,19},{19,3},{4,20},{20... | collective-permute-start | bytes 3932168 | tf_op jit(solution)/shard_map/ppermute | solution.py:121
  35.7 22.8 %copy-start.2 = (bf16[8,8,2048]{2,1,0:T(8,128)(2,1)}, bf16[8,8,2048]{2,1,0:T(8,128)(2,1)S(1)}, u32[]{:S(2)}) copy-start(bf16[8,8,2048]{2,1,0:T(8,128)(2,1)S(1)} %all-to-all-done) | copy-start | bytes 786436
  36.4 13.4 %collective-permute-start.3 = (bf16[2,16,2048]{2,1,0:T(8,128)(2,1)S(1)}, bf16[2,16,2048]{2,1,0:T(8,128)(2,1)S(1)}, u32[]{:S(2)}, u32[]{:S(2)}) collective-permute-start(bf16[2,16,2048]{2,1,0:T(8,128)(2,1)S(1)} %get-tuple-element.12), channel_id=1, source_target_pairs={{0,14},{1,15},{2,0},{3,1},{4,2},{5,3},{6,4},{7,5},{8,6},{9,7},{10,... | collective-permute-start | bytes 393224 | tf_op jit(solution)/shard_map/ppermute | solution.py:108
  43.3 15.1 %collective-permute-start.1 = (bf16[2,32,2048]{2,1,0:T(8,128)(2,1)S(1)}, bf16[2,32,2048]{2,1,0:T(8,128)(2,1)S(1)}, u32[]{:S(2)}, u32[]{:S(2)}) collective-permute-start(bf16[2,32,2048]{2,1,0:T(8,128)(2,1)S(1)} %bitcast.16), channel_id=1, source_target_pairs={{0,15},{1,0},{2,1},{3,2},{4,3},{5,4},{6,5},{7,6},{8,7},{9,8},{10,9... | collective-permute-start | bytes 786440 | tf_op jit(solution)/shard_map/ppermute | solution.py:106
  45.2 13.1 %collective-permute-start = (bf16[2,32,2048]{2,1,0:T(8,128)(2,1)S(1)}, bf16[2,32,2048]{2,1,0:T(8,128)(2,1)S(1)}, u32[]{:S(2)}, u32[]{:S(2)}) collective-permute-start(bf16[2,32,2048]{2,1,0:T(8,128)(2,1)S(1)} %bitcast.17), channel_id=1, source_target_pairs={{0,1},{1,2},{2,3},{3,4},{4,5},{5,6},{6,7},{7,8},{8,9},{9,10},{10,1... | collective-permute-start | bytes 786440 | tf_op jit(solution)/shard_map/ppermute | solution.py:105
  49.8 8.6 %copy-start.7 = (bf16[2,16,2048]{2,1,0:T(8,128)(2,1)}, bf16[2,16,2048]{2,1,0:T(8,128)(2,1)S(1)}, u32[]{:S(2)}) copy-start(bf16[2,16,2048]{2,1,0:T(8,128)(2,1)S(1)} %collective-permute-done.3.high) | copy-start | bytes 393220
  49.8 8.5 %collective-permute-start.2 = (bf16[2,16,2048]{2,1,0:T(8,128)(2,1)}, bf16[2,16,2048]{2,1,0:T(8,128)(2,1)}, u32[]{:S(2)}, u32[]{:S(2)}) collective-permute-start(bf16[2,16,2048]{2,1,0:T(8,128)(2,1)} %get-tuple-element.13), channel_id=1, source_target_pairs={{0,2},{1,3},{2,4},{3,5},{4,6},{5,7},{6,8},{7,9},{8,10},{9,11},{10,... | collective-permute-start | bytes 393224 | tf_op jit(solution)/shard_map/ppermute | solution.py:107
  58.4 0.7 copy-start.4
  58.4 0.8 copy-start.5
  64.3 16.2 %copy-start.8 = (f32[2048]{0:T(1024)S(1)}, f32[2048]{0:T(1024)}, u32[]{:S(2)}) copy-start(f32[2048]{0:T(1024)} %param.6) | copy-start | bytes 24580
  80.5 19.3 %copy-start.6 = (f32[8,2048]{1,0:T(8,128)}, f32[8,2048]{1,0:T(8,128)S(1)}, u32[]{:S(2)}) copy-start(f32[8,2048]{1,0:T(8,128)S(1)} %convert_reduce_fusion) | copy-start | bytes 196612
  81.4 12.6 %all-to-all-start.2 = ((bf16[16,8,2048]{2,1,0:T(8,128)(2,1)}), bf16[16,8,2048]{2,1,0:T(8,128)(2,1)S(1)}, u32[]{:S(2)}, u32[]{:S(2)}) async-start(bf16[16,8,2048]{2,1,0:T(8,128)(2,1)} %broadcast_in_dim.27), calls=%async_computation.2 | async-start | bytes 1048576 | tf_op jit(solution)/shard_map/all_to_all | solution.py:100
  93.9 0.8 copy-start.3
  99.8 18.3 %collective-permute-start.6 = (bf16[2,4,128,128]{3,2,1,0:T(8,128)(2,1)}, bf16[2,4,128,128]{3,2,1,0:T(8,128)(2,1)S(1)}, u32[]{:S(2)}, u32[]{:S(2)}) collective-permute-start(bf16[2,4,128,128]{3,2,1,0:T(8,128)(2,1)} %get-tuple-element.8), channel_id=1, source_target_pairs={{0,1},{1,2},{2,3},{3,4},{4,5},{5,6},{6,7},{7,8},{8,9},{9,10},{10,1... | collective-permute-start | bytes 786440 | tf_op jit(solution)/shard_map/ppermute | solution.py:105
  103.9 14.2 %collective-permute-start.7 = (bf16[2,4,128,128]{3,2,1,0:T(8,128)(2,1)}, bf16[2,4,128,128]{3,2,1,0:T(8,128)(2,1)S(1)}, u32[]{:S(2)}, u32[]{:S(2)}) collective-permute-start(bf16[2,4,128,128]{3,2,1,0:T(8,128)(2,1)} %get-tuple-element.9), channel_id=1, source_target_pairs={{0,15},{1,0},{2,1},{3,2},{4,3},{5,4},{6,5},{7,6},{8,7},{9,8},{10,9... | collective-permute-start | bytes 786440 | tf_op jit(solution)/shard_map/ppermute | solution.py:106
  105.9 10.1 %collective-permute-start.8 = (bf16[2,2,128,128]{3,2,1,0:T(8,128)(2,1)}, bf16[2,2,128,128]{3,2,1,0:T(8,128)(2,1)S(1)}, u32[]{:S(2)}, u32[]{:S(2)}) collective-permute-start(bf16[2,2,128,128]{3,2,1,0:T(8,128)(2,1)} %get-tuple-element.10), channel_id=1, source_target_pairs={{0,2},{1,3},{2,4},{3,5},{4,6},{5,7},{6,8},{7,9},{8,10},{9,11},{10,... | collective-permute-start | bytes 393224 | tf_op jit(solution)/shard_map/ppermute | solution.py:107
  109.8 8.3 %collective-permute-start.9 = (bf16[2,2,128,128]{3,2,1,0:T(8,128)(2,1)}, bf16[2,2,128,128]{3,2,1,0:T(8,128)(2,1)S(1)}, u32[]{:S(2)}, u32[]{:S(2)}) collective-permute-start(bf16[2,2,128,128]{3,2,1,0:T(8,128)(2,1)} %get-tuple-element.11), channel_id=1, source_target_pairs={{0,14},{1,15},{2,0},{3,1},{4,2},{5,3},{6,4},{7,5},{8,6},{9,7},{10,... | collective-permute-start | bytes 393224 | tf_op jit(solution)/shard_map/ppermute | solution.py:108

commit v2 on v1

v2 whole, which is shorter than its diff:
```python
import functools

import jax
import jax.numpy as jnp
from jax import lax
from jax.experimental import pallas as pl
from jax.experimental.pallas import tpu as pltpu
from jax.sharding import Mesh
from jax.sharding import PartitionSpec as P

LINE = ("zh", "zl")
PAIR_LINE = ("c", "zh", "zl")
NT = (((1,), (1,)), ((), ()))
TN = (((0,), (0,)), ((), ()))
STEPS = (0, -5, 5, -1, -6, 4, 1, -4, 6, -2, -7, 3, 2, -3, 7, -8)


def turned(x, steps):
    pairs = [
        (c * 16 + z, c * 16 + (z + (steps if c == 0 else -steps)) % 16)
        for c in range(2)
        for z in range(16)
    ]
    return lax.ppermute(x, PAIR_LINE, pairs)


def forward_kernel(home, p0, p1, p2, p3, p4, p5, v0, v1, u0, u1, out, x, coeffs):
    for s in range(16):
        block = p5 if s == 15 else (p0, p1, p2, p3, p4)[s // 3].at[s % 3]
        for k in range(2):
            x[k, home[s]] = block[k]
    for k, v in enumerate((v0, v1)):
        for j in range(4):
            xj = x[k, :, :, pl.ds(j * 512, 512)].reshape(128, 512)
            tall = jnp.concatenate([v[i, j] for i in range(4)], 0)
            c = lax.dot_general(tall, xj, NT, preferred_element_type=jnp.float32)
            for i in range(4):
                coeffs[i, pl.ds(k * 320 + j * 80, 80), :] = c[i * 80 : i * 80 + 80].astype(jnp.bfloat16)
    for i in range(4):
        u = jnp.concatenate([u[i, j] for u in (u0, u1) for j in range(4)], 0)
        part = lax.dot_general(coeffs[i], u, TN, preferred_element_type=jnp.float32)
        out[:, :, pl.ds(i * 512, 512)] = part.reshape(16, 8, 512).astype(jnp.bfloat16)


def adjoint_kernel(home, w, v0, v1, u0, u1, p0, p1, p2, p3, p4, p5, coeffs, blocks):
    for k, u in enumerate((u0, u1)):
        for i in range(4):
            tall = jnp.concatenate([u[i, j] for j in range(4)], 0)
            a = lax.dot_general(tall, w[:, pl.ds(i * 512, 512)], NT, preferred_element_type=jnp.float32)
            for j in range(4):
                coeffs[k, j, pl.ds(i * 80, 80), :] = a[j * 80 : j * 80 + 80].astype(jnp.bfloat16)
    for k, v in enumerate((v0, v1)):
        for j in range(4):
            tall = jnp.concatenate([v[i, j] for i in range(4)], 0)
            back = lax.dot_general(coeffs[k, j], tall, TN, preferred_element_type=jnp.float32)
            back = back.astype(jnp.bfloat16)
            for q in range(4):
                blocks[4 * j + q, k] = back[:, q * 128 : q * 128 + 128]
    for s in range(16):
        block = p5 if s == 15 else (p0, p1, p2, p3, p4)[s // 3].at[s % 3]
        block[...] = blocks[home[s]]


SMEM = pl.BlockSpec(memory_space=pltpu.SMEM)
VMEM = pl.BlockSpec(memory_space=pltpu.VMEM)
ROOM = pltpu.CompilerParams(vmem_limit_bytes=20 * 1024 * 1024)


def forward_part(home, pieces, v, u):
    return pl.pallas_call(
        forward_kernel,
        out_shape=jax.ShapeDtypeStruct((16, 8, 2048), jnp.bfloat16),
        in_specs=[SMEM] + [VMEM] * 10,
        out_specs=VMEM,
        scratch_shapes=[
            pltpu.VMEM((2, 16, 8, 2048), jnp.bfloat16),
            pltpu.VMEM((4, 640, 128), jnp.bfloat16),
        ],
        compiler_params=ROOM,
        name="forward_part",
    )(home, *pieces, *v, *u)


def adjoint_part(home, weighted, v, u):
    three = jax.ShapeDtypeStruct((3, 2, 128, 128), jnp.bfloat16)
    single = jax.ShapeDtypeStruct((2, 128, 128), jnp.bfloat16)
    return pl.pallas_call(
        adjoint_kernel,
        out_shape=(three,) * 5 + (single,),
        in_specs=[SMEM] + [VMEM] * 5,
        out_specs=(VMEM,) * 6,
        scratch_shapes=[
            pltpu.VMEM((2, 4, 320, 128), jnp.bfloat16),
            pltpu.VMEM((16, 2, 128, 128), jnp.bfloat16),
        ],
        compiler_params=ROOM,
        name="adjoint_part",
    )(home, weighted, *v, *u)


def exchange(blocks, axes):
    return lax.all_to_all(blocks, axes, split_axis=0, concat_axis=0, tiled=True)


def line_gather(block):
    back = turned(block, 5)
    ahead = turned(block, -5)
    three = jnp.stack([block, back, ahead])
    return (
        three,
        turned(three, 1),
        turned(three, -1),
        turned(three, 2),
        turned(three, -2),
        turned(back, 3),
    )


def line_sum(p0, p1, p2, p3, p4, p5):
    near = [turned(p1, -1), turned(p2, 1), turned(p3, -2), turned(p4, 2)]
    half_way = turned(p5, -3)
    total = p0.astype(jnp.float32)
    for blocks in near:
        total = total + blocks.astype(jnp.float32)
    behind = (total[1] + half_way.astype(jnp.float32)).astype(jnp.bfloat16)
    ahead = total[2].astype(jnp.bfloat16)
    own = total[0]
    return own + turned(behind, -5).astype(jnp.float32) + turned(ahead, 5).astype(jnp.float32)


def both_products(samples, row_weights, tile_ranks, u_factors, v_factors):
    core = lax.axis_index("c")
    swap = functools.partial(lax.ppermute, axis_name="c", perm=[(0, 1), (1, 0)])
    home = (lax.axis_index(LINE) + (1 - 2 * core) * jnp.array(STEPS, jnp.int32)) & 15

    x = samples.astype(jnp.bfloat16).reshape(2, 8, 2048)
    kept = lax.dynamic_index_in_dim(x, core, 0, keepdims=False)
    given = lax.dynamic_index_in_dim(x, 1 - core, 0, keepdims=False)
    block = jnp.stack([kept, swap(given)])
    block, u_factors, v_factors = lax.optimization_barrier((block, u_factors, v_factors))
    pieces = line_gather(block)
    levels = lax.broadcasted_iota(jnp.int32, (1, 1, 80, 1), 2)
    ranked = jnp.where(levels < tile_ranks[:, :, None, None], u_factors, jnp.zeros_like(u_factors))
    v = (v_factors, swap(v_factors))
    u = (ranked, swap(ranked))

    part = forward_part(home, pieces, v, u)
    forward_rows = jnp.sum(exchange(part, ("xy",)).astype(jnp.float32), axis=0)

    weighted = (forward_rows * row_weights[None, :]).astype(jnp.bfloat16)
    weighted = exchange(jnp.broadcast_to(weighted, (16, 8, 2048)), ("xy",)).reshape(128, 2048)

    own, other = line_sum(*adjoint_part(home, weighted, v, u))
    got = swap(other)
    even = jnp.where(core == 0, own, got).reshape(16, 1, 8, 128)
    odd = jnp.where(core == 0, got, own).reshape(16, 1, 8, 128)
    adjoint_cols = jnp.concatenate([even, odd], 1).reshape(256, 128)
    return forward_rows, adjoint_cols


def solution(mesh):
    fine = Mesh(mesh.devices.reshape(16, 2, 4, 4), ("xy", "c", "zh", "zl"))
    narrow, wide = LINE, ("xy", "c")
    in_specs = (
        P(narrow, wide),
        P(narrow),
        P(narrow, wide),
        P(narrow, wide, None, None),
        P(narrow, wide, None, None),
    )
    out_specs = (P(wide, narrow), P(None, (*wide, *narrow)))
    return jax.shard_map(both_products, mesh=fine, in_specs=in_specs, out_specs=out_specs, check_vma=False)
```

time: 149 us -> 144 us (0.966)
  starting transfers between devices: 54.7 us -> 78.5 us
  blocking collectives: 44 us -> 27.7 us
  local copies, waits for them, and re-layouts: 5.75 us -> 0.76 us
  Pallas kernels: 10.1 us -> 6.42 us
  waiting for transfers between devices: 27.8 us -> 25.4 us
    ppermute x10 -> x18, starting transfers between devices: 34.5 us -> 78.5 us  [the longest x14 58.6 us: turned(): return lax.ppermute(x, PAIR_LINE, pairs)]
    all_to_all x2 -> x0, starting transfers between devices: 20.2 us -> none  [exchange(): return lax.all_to_all(blocks, axes, split_axis=0, concat_axis=0, tiled=True)]
    all_to_all x2 -> x0, waiting for transfers between devices: 18.4 us -> none  [exchange(): return lax.all_to_all(blocks, axes, split_axis=0, concat_axis=0, tiled=True)]
    all_to_all x2, blocking collectives: 44 us -> 27.7 us  [exchange(): return lax.all_to_all(blocks, axes, split_axis=0, concat_axis=0, tiled=True)]
    ppermute x10 -> x18, waiting for transfers between devices: 9.36 us -> 25.4 us  [the longest x14 24.4 us: turned(): return lax.ppermute(x, PAIR_LINE, pairs)]
    pallas_call x1, Pallas kernels: 5.05 us -> 3.17 us  [forward_part(): pl.pallas_call(forward_kernel, out_shape=jax.ShapeDtypeStruct((16, 8, 204...]
    pallas_call x1, Pallas kernels: 5.09 us -> 3.25 us  [adjoint_part(): pl.pallas_call(adjoint_kernel, out_shape=(three,) * 5 + (single,), in_spe...]
    unnamed x18 -> x8, local copies, waits for them, and re-layouts: 1.59 us -> 0.02 us
  transfers between devices with their start and end apart: 12 -> 18, of which waited for: 5 -> 9; matrix products, arithmetic and copies ran while one was open for 3% -> 1% of each run, Pallas kernels for 0% -> 0%
where the time goes in v2:
time: 144 us; the launch traced here: 143 us
  starting transfers between devices  78.5 us (55%)
  blocking collectives  27.7 us (19%)
  waiting for transfers between devices  25.4 us (18%)
  Pallas kernels  6.42 us (4%)
  other arithmetic  3.64 us (3%)
    ppermute x14, starting transfers between devices, turned(): return lax.ppermute(x, PAIR_LINE, pairs)  58.6 us
    all_to_all x2, blocking collectives, exchange(): return lax.all_to_all(blocks, axes, split_axis=0, concat_axis=0, tiled=True)  27.7 us
    ppermute x14, waiting for transfers between devices, turned(): return lax.ppermute(x, PAIR_LINE, pairs)  24.4 us
    ppermute x1, starting transfers between devices, both_products(): block = jnp.stack([kept, swap(given)])  8.75 us
    ppermute x1, starting transfers between devices, both_products(): got = swap(other)  6.78 us
    pallas_call x1, Pallas kernels, adjoint_part(): pl.pallas_call(adjoint_kernel, out_shape=(three,) * 5 + (single,), in_spe...  3.25 us
    pallas_call x1, Pallas kernels, forward_part(): pl.pallas_call(forward_kernel, out_shape=jax.ShapeDtypeStruct((16, 8, 204...  3.17 us
  transfers between devices with their start and end apart: 18, of which 9 were waited for; matrix products, arithmetic and copies ran while one was open for 1% of the time, Pallas kernels for 0%

profile of v2, /device:TPU:1, one launch (start us, length us, event | category | flops | bytes accessed | tf_op | source)
XLA Modules:
  0.0 143.4 jit_solution(6058793014389094697)
XLA Ops:
  1.6 8.7 %collective-permute-start = (bf16[8,2048]{1,0:T(8,128)(2,1)S(1)}, bf16[8,2048]{1,0:T(8,128)(2,1)S(1)}, u32[]{:S(2)}, u32[]{:S(2)}) collective-permute-start(bf16[8,2048]{1,0:T(8,128)(2,1)S(1)} %get-tuple-element.23), channel_id=1, source_target_pairs={{0,16},{16,0},{1,17},{17,1},{2,18},{18,2},{3,19},{19,3},{4,20},{20... | collective-permute-start | bytes 98312 | tf_op jit(solution)/shard_map/ppermute | solution.py:139
  12.8 2.3 %collective-permute-start.9 = (bf16[4,4,80,512]{3,2,1,0:T(8,128)(2,1)S(1)}, bf16[4,4,80,512]{3,2,1,0:T(8,128)(2,1)}, u32[]{:S(2)}, u32[]{:S(2)}) collective-permute-start(bf16[4,4,80,512]{3,2,1,0:T(8,128)(2,1)S(1)} %broadcast_select_fusion.u0), channel_id=1, source_target_pairs={{0,16},{16,0},{1,17},{17,1},{2,18},{18,2},{3,19},{19,3},{4,20},{20... | collective-permute-start | bytes 3932168 | tf_op jit(solution)/shard_map/ppermute | solution.py:145
  17.2 4.8 %collective-permute-start.2 = (bf16[2,8,2048]{2,1,0:T(8,128)(2,1)S(1)}, bf16[2,8,2048]{2,1,0:T(8,128)(2,1)S(1)}, u32[]{:S(2)}, u32[]{:S(2)}) collective-permute-start(bf16[2,8,2048]{2,1,0:T(8,128)(2,1)S(1)} %pad_maximum_fusion.2), channel_id=1, source_target_pairs={{0,11},{1,12},{2,13},{3,14},{4,15},{5,0},{6,1},{7,2},{8,3},{9,4},{... | collective-permute-start | bytes 196616 | tf_op jit(solution)/shard_map/ppermute | solution.py:24
  22.0 6.5 %collective-permute-start.1 = (bf16[2,8,2048]{2,1,0:T(8,128)(2,1)S(1)}, bf16[2,8,2048]{2,1,0:T(8,128)(2,1)S(1)}, u32[]{:S(2)}, u32[]{:S(2)}) collective-permute-start(bf16[2,8,2048]{2,1,0:T(8,128)(2,1)S(1)} %pad_maximum_fusion.2), channel_id=1, source_target_pairs={{0,5},{1,6},{2,7},{3,8},{4,9},{5,10},{6,11},{7,12},{8,13},{9,14},{... | collective-permute-start | bytes 196616 | tf_op jit(solution)/shard_map/ppermute | solution.py:24
  28.5 5.6 %collective-permute-done.1 = bf16[2,8,2048]{2,1,0:T(8,128)(2,1)S(1)} collective-permute-done((bf16[2,8,2048]{2,1,0:T(8,128)(2,1)S(1)}, bf16[2,8,2048]{2,1,0:T(8,128)(2,1)S(1)}, u32[]{:S(2)}, u32[]{:S(2)}) %collective-permute-start.1) | collective-permute-done | bytes 65568 | tf_op jit(solution)/shard_map/ppermute | solution.py:24
  34.2 2.6 %collective-permute-start.6 = (bf16[3,2,8,2048]{3,2,1,0:T(8,128)(2,1)S(1)}, bf16[3,2,8,2048]{3,2,1,0:T(8,128)(2,1)S(1)}, u32[]{:S(2)}, u32[]{:S(2)}) collective-permute-start(bf16[3,2,8,2048]{3,2,1,0:T(8,128)(2,1)S(1)} %pad_maximum_fusion.p0), channel_id=1, source_target_pairs={{0,14},{1,15},{2,0},{3,1},{4,2},{5,3},{6,4},{7,5},{8,6},{9,7},{10,... | collective-permute-start | bytes 589832 | tf_op jit(solution)/shard_map/ppermute | solution.py:24
  36.8 4.9 %collective-permute-start.7 = (bf16[2,8,2048]{2,1,0:T(8,128)(2,1)S(1)}, bf16[2,8,2048]{2,1,0:T(8,128)(2,1)S(1)}, u32[]{:S(2)}, u32[]{:S(2)}) collective-permute-start(bf16[2,8,2048]{2,1,0:T(8,128)(2,1)S(1)} %collective-permute-done.1), channel_id=1, source_target_pairs={{0,3},{1,4},{2,5},{3,6},{4,7},{5,8},{6,9},{7,10},{8,11},{9,12},{10... | collective-permute-start | bytes 196616 | tf_op jit(solution)/shard_map/ppermute | solution.py:24
  41.7 6.6 %collective-permute-start.5 = (bf16[3,2,8,2048]{3,2,1,0:T(8,128)(2,1)S(1)}, bf16[3,2,8,2048]{3,2,1,0:T(8,128)(2,1)S(1)}, u32[]{:S(2)}, u32[]{:S(2)}) collective-permute-start(bf16[3,2,8,2048]{3,2,1,0:T(8,128)(2,1)S(1)} %pad_maximum_fusion.p0), channel_id=1, source_target_pairs={{0,2},{1,3},{2,4},{3,5},{4,6},{5,7},{6,8},{7,9},{8,10},{9,11},{10,... | collective-permute-start | bytes 589832 | tf_op jit(solution)/shard_map/ppermute | solution.py:24
  48.3 3.9 %collective-permute-start.4 = (bf16[3,2,8,2048]{3,2,1,0:T(8,128)(2,1)S(1)}, bf16[3,2,8,2048]{3,2,1,0:T(8,128)(2,1)S(1)}, u32[]{:S(2)}, u32[]{:S(2)}) collective-permute-start(bf16[3,2,8,2048]{3,2,1,0:T(8,128)(2,1)S(1)} %pad_maximum_fusion.p0), channel_id=1, source_target_pairs={{0,15},{1,0},{2,1},{3,2},{4,3},{5,4},{6,5},{7,6},{8,7},{9,8},{10,9... | collective-permute-start | bytes 589832 | tf_op jit(solution)/shard_map/ppermute | solution.py:24
  52.3 2.6 %collective-permute-start.3 = (bf16[3,2,8,2048]{3,2,1,0:T(8,128)(2,1)S(1)}, bf16[3,2,8,2048]{3,2,1,0:T(8,128)(2,1)S(1)}, u32[]{:S(2)}, u32[]{:S(2)}) collective-permute-start(bf16[3,2,8,2048]{3,2,1,0:T(8,128)(2,1)S(1)} %pad_maximum_fusion.p0), channel_id=1, source_target_pairs={{0,1},{1,2},{2,3},{3,4},{4,5},{5,6},{6,7},{7,8},{8,9},{9,10},{10,1... | collective-permute-start | bytes 589832 | tf_op jit(solution)/shard_map/ppermute | solution.py:24
  55.6 3.1 %collective-permute-done.4.p2 = bf16[3,2,8,2048]{3,2,1,0:T(8,128)(2,1)S(1)} collective-permute-done((bf16[3,2,8,2048]{3,2,1,0:T(8,128)(2,1)S(1)}, bf16[3,2,8,2048]{3,2,1,0:T(8,128)(2,1)S(1)}, u32[]{:S(2)}, u32[]{:S(2)}) %collective-permute-start.4) | collective-permute-done | bytes 196640 | tf_op jit(solution)/shard_map/ppermute | solution.py:24
  58.7 2.7 %collective-permute-done.3.p1 = bf16[3,2,8,2048]{3,2,1,0:T(8,128)(2,1)S(1)} collective-permute-done((bf16[3,2,8,2048]{3,2,1,0:T(8,128)(2,1)S(1)}, bf16[3,2,8,2048]{3,2,1,0:T(8,128)(2,1)S(1)}, u32[]{:S(2)}, u32[]{:S(2)}) %collective-permute-start.3) | collective-permute-done | bytes 196640 | tf_op jit(solution)/shard_map/ppermute | solution.py:24
  61.4 3.2 %forward_part.1 = bf16[16,8,2048]{2,1,0:T(8,128)(2,1)S(1)} custom-call(s32[16]{0:T(128)S(1)} %add_and_fusion.home, bf16[3,2,8,2048]{3,2,1,0:T(8,128)(2,1)S(1)} %pad_maximum_fusion.p0, bf16[3,2,8,2048]{3,2,1,0:T(8,128)(2,1)S(1)} %collective-permute-done.3.p1, bf16[3,2,8,2048]{3,2,1,0:T(8,128)(2,1)S(1)} %collective-permute-done.4.p2, ...), custom_call_target="tpu_custom_call" | custom-call | tf_op jit(solution)/shard_map/forward_part/pallas_call | solution.py:70
  64.6 15.7 %all_to_all.10 = bf16[16,8,2048]{2,1,0:T(8,128)(2,1)S(1)} all-to-all(bf16[16,8,2048]{2,1,0:T(8,128)(2,1)S(1)} %forward_part.1), channel_id=1, replica_groups=mesh['xy'=16,'c'=2,'zh'=4,'zl'=4] {'xy'}, dimensions={0} | all-to-all | bytes 1048576 | tf_op jit(solution)/shard_map/all_to_all | solution.py:102
  80.4 12.1 %all_to_all.11 = bf16[16,8,2048]{2,1,0:T(8,128)(2,1)S(1)} all-to-all(bf16[16,8,2048]{2,1,0:T(8,128)(2,1)S(1)} %broadcast_in_dim.18), channel_id=1, replica_groups=mesh['xy'=16,'c'=2,'zh'=4,'zl'=4] {'xy'}, dimensions={0} | all-to-all | bytes 1048576 | tf_op jit(solution)/shard_map/all_to_all | solution.py:102
  92.5 3.2 %adjoint_part.1 = (bf16[3,2,128,128]{3,2,1,0:T(8,128)(2,1)S(1)}, bf16[3,2,128,128]{3,2,1,0:T(8,128)(2,1)S(1)}, bf16[3,2,128,128]{3,2,1,0:T(8,128)(2,1)S(1)}, bf1...) custom-call(s32[16]{0:T(128)S(1)} %add_and_fusion.home, ...), custom_call_target="tpu_custom_call" | custom-call | tf_op jit(solution)/shard_map/adjoint_part/pallas_call | solution.py:87
  95.8 5.4 %collective-permute-start.10 = (bf16[3,2,128,128]{3,2,1,0:T(8,128)(2,1)S(1)}, bf16[3,2,128,128]{3,2,1,0:T(8,128)(2,1)S(1)}, u32[]{:S(2)}, u32[]{:S(2)}) collective-permute-start(bf16[3,2,128,128]{3,2,1,0:T(8,128)(2,1)S(1)} %get-tuple-element.15), channel_id=1, source_target_pairs={{0,15},{1,0},{2,1},{3,2},{4,3},{5,4},{6,5},{7,6},{8,7},{9,8},{10,9... | collective-permute-start | bytes 589832 | tf_op jit(solution)/shard_map/ppermute | solution.py:24
  103.1 3.1 %collective-permute-start.12 = (bf16[3,2,128,128]{3,2,1,0:T(8,128)(2,1)S(1)}, bf16[3,2,128,128]{3,2,1,0:T(8,128)(2,1)S(1)}, u32[]{:S(2)}, u32[]{:S(2)}) collective-permute-start(bf16[3,2,128,128]{3,2,1,0:T(8,128)(2,1)S(1)} %get-tuple-element.17), channel_id=1, source_target_pairs={{0,14},{1,15},{2,0},{3,1},{4,2},{5,3},{6,4},{7,5},{8,6},{9,7},{10,... | collective-permute-start | bytes 589832 | tf_op jit(solution)/shard_map/ppermute | solution.py:24
  106.2 4.3 %collective-permute-start.13 = (bf16[3,2,128,128]{3,2,1,0:T(8,128)(2,1)S(1)}, bf16[3,2,128,128]{3,2,1,0:T(8,128)(2,1)S(1)}, u32[]{:S(2)}, u32[]{:S(2)}) collective-permute-start(bf16[3,2,128,128]{3,2,1,0:T(8,128)(2,1)S(1)} %get-tuple-element.18), channel_id=1, source_target_pairs={{0,2},{1,3},{2,4},{3,5},{4,6},{5,7},{6,8},{7,9},{8,10},{9,11},{10,... | collective-permute-start | bytes 589832 | tf_op jit(solution)/shard_map/ppermute | solution.py:24
  114.4 5.7 %collective-permute-done.13 = bf16[3,2,128,128]{3,2,1,0:T(8,128)(2,1)S(1)} collective-permute-done((bf16[3,2,128,128]{3,2,1,0:T(8,128)(2,1)S(1)}, bf16[3,2,128,128]{3,2,1,0:T(8,128)(2,1)S(1)}, u32[]{:S(2)}, u32[]{:S(2)}) %collective-permute-start.13) | collective-permute-done | bytes 196640 | tf_op jit(solution)/shard_map/ppermute | solution.py:24
  120.3 3.4 %collective-permute-start.16 = (bf16[2,128,128]{2,1,0:T(8,128)(2,1)S(1)}, bf16[2,128,128]{2,1,0:T(8,128)(2,1)S(1)}, u32[]{:S(2)}, u32[]{:S(2)}) collective-permute-start(bf16[2,128,128]{2,1,0:T(8,128)(2,1)S(1)} %fusion.4), channel_id=1, source_target_pairs={{0,5},{1,6},{2,7},{3,8},{4,9},{5,10},{6,11},{7,12},{8,13},{9,14},{... | collective-permute-start | bytes 196616 | tf_op jit(solution)/shard_map/ppermute | solution.py:24
  123.8 6.7 %collective-permute-start.15 = (bf16[2,128,128]{2,1,0:T(8,128)(2,1)S(1)}, bf16[2,128,128]{2,1,0:T(8,128)(2,1)S(1)}, u32[]{:S(2)}, u32[]{:S(2)}) collective-permute-start(bf16[2,128,128]{2,1,0:T(8,128)(2,1)S(1)} %fusion.1), channel_id=1, source_target_pairs={{0,11},{1,12},{2,13},{3,14},{4,15},{5,0},{6,1},{7,2},{8,3},{9,4},{... | collective-permute-start | bytes 196616 | tf_op jit(solution)/shard_map/ppermute | solution.py:24
  130.4 4.6 %collective-permute-done.15 = bf16[2,128,128]{2,1,0:T(8,128)(2,1)S(1)} collective-permute-done((bf16[2,128,128]{2,1,0:T(8,128)(2,1)S(1)}, bf16[2,128,128]{2,1,0:T(8,128)(2,1)S(1)}, u32[]{:S(2)}, u32[]{:S(2)}) %collective-permute-start.15) | collective-permute-done | bytes 65568 | tf_op jit(solution)/shard_map/ppermute | solution.py:24
  135.0 6.8 %collective-permute-start.17 = (f32[128,128]{1,0:T(8,128)S(1)}, f32[128,128]{1,0:T(8,128)S(1)}, u32[]{:S(2)}, u32[]{:S(2)}) collective-permute-start(f32[128,128]{1,0:T(8,128)S(1)} %slice_bitcast_fusion.2), channel_id=1, source_target_pairs={{0,16},{16,0},{1,17},{17,1},{2,18},{18,2},{3,19},{19,3},{4,20},{20... | collective-permute-start | bytes 196616 | tf_op jit(solution)/shard_map/ppermute | solution.py:154
  (42 shorter events, 13.9 us)
Async XLA Ops:
  1.6 9.6 %collective-permute-start = (bf16[8,2048]{1,0:T(8,128)(2,1)S(1)}, bf16[8,2048]{1,0:T(8,128)(2,1)S(1)}, u32[]{:S(2)}, u32[]{:S(2)}) collective-permute-start(bf16[8,2048]{1,0:T(8,128)(2,1)S(1)} %get-tuple-element.23), channel_id=1, source_target_pairs={{0,16},{16,0},{1,17},{17,1},{2,18},{18,2},{3,19},{19,3},{4,20},{20... | collective-permute-start | bytes 98312 | tf_op jit(solution)/shard_map/ppermute | solution.py:139
  11.2 4.0 %copy-start = (bf16[4,4,80,512]{3,2,1,0:T(8,128)(2,1)S(1)}, bf16[4,4,80,512]{3,2,1,0:T(8,128)(2,1)}, u32[]{:S(2)}) copy-start(bf16[4,4,80,512]{3,2,1,0:T(8,128)(2,1)} %v0.1) | copy-start | bytes 3932164
  11.2 43.7 %copy-start.3 = (s32[16]{0:T(128)S(1)}, s32[16]{0:T(128)}, u32[]{:S(2)}) copy-start(s32[16]{0:T(128)} %constant.37.clone) | copy-start | bytes 196
  12.8 48.6 %collective-permute-start.9 = (bf16[4,4,80,512]{3,2,1,0:T(8,128)(2,1)S(1)}, bf16[4,4,80,512]{3,2,1,0:T(8,128)(2,1)}, u32[]{:S(2)}, u32[]{:S(2)}) collective-permute-start(bf16[4,4,80,512]{3,2,1,0:T(8,128)(2,1)S(1)} %broadcast_select_fusion.u0), channel_id=1, source_target_pairs={{0,16},{16,0},{1,17},{17,1},{2,18},{18,2},{3,19},{19,3},{4,20},{20... | collective-permute-start | bytes 3932168 | tf_op jit(solution)/shard_map/ppermute | solution.py:145
  15.1 46.3 %collective-permute-start.8 = (bf16[4,4,80,512]{3,2,1,0:T(8,128)(2,1)S(1)}, bf16[4,4,80,512]{3,2,1,0:T(8,128)(2,1)}, u32[]{:S(2)}, u32[]{:S(2)}) collective-permute-start(bf16[4,4,80,512]{3,2,1,0:T(8,128)(2,1)S(1)} %copy-done), channel_id=1, source_target_pairs={{0,16},{16,0},{1,17},{17,1},{2,18},{18,2},{3,19},{19,3},{4,20},{20... | collective-permute-start | bytes 3932168 | tf_op jit(solution)/shard_map/ppermute | solution.py:144
  17.2 11.3 %collective-permute-start.2 = (bf16[2,8,2048]{2,1,0:T(8,128)(2,1)S(1)}, bf16[2,8,2048]{2,1,0:T(8,128)(2,1)S(1)}, u32[]{:S(2)}, u32[]{:S(2)}) collective-permute-start(bf16[2,8,2048]{2,1,0:T(8,128)(2,1)S(1)} %pad_maximum_fusion.2), channel_id=1, source_target_pairs={{0,11},{1,12},{2,13},{3,14},{4,15},{5,0},{6,1},{7,2},{8,3},{9,4},{... | collective-permute-start | bytes 196616 | tf_op jit(solution)/shard_map/ppermute | solution.py:24
  22.0 12.1 %collective-permute-start.1 = (bf16[2,8,2048]{2,1,0:T(8,128)(2,1)S(1)}, bf16[2,8,2048]{2,1,0:T(8,128)(2,1)S(1)}, u32[]{:S(2)}, u32[]{:S(2)}) collective-permute-start(bf16[2,8,2048]{2,1,0:T(8,128)(2,1)S(1)} %pad_maximum_fusion.2), channel_id=1, source_target_pairs={{0,5},{1,6},{2,7},{3,8},{4,9},{5,10},{6,11},{7,12},{8,13},{9,14},{... | collective-permute-start | bytes 196616 | tf_op jit(solution)/shard_map/ppermute | solution.py:24
  34.2 18.1 %collective-permute-start.6 = (bf16[3,2,8,2048]{3,2,1,0:T(8,128)(2,1)S(1)}, bf16[3,2,8,2048]{3,2,1,0:T(8,128)(2,1)S(1)}, u32[]{:S(2)}, u32[]{:S(2)}) collective-permute-start(bf16[3,2,8,2048]{3,2,1,0:T(8,128)(2,1)S(1)} %pad_maximum_fusion.p0), channel_id=1, source_target_pairs={{0,14},{1,15},{2,0},{3,1},{4,2},{5,3},{6,4},{7,5},{8,6},{9,7},{10,... | collective-permute-start | bytes 589832 | tf_op jit(solution)/shard_map/ppermute | solution.py:24
  36.8 11.5 %collective-permute-start.7 = (bf16[2,8,2048]{2,1,0:T(8,128)(2,1)S(1)}, bf16[2,8,2048]{2,1,0:T(8,128)(2,1)S(1)}, u32[]{:S(2)}, u32[]{:S(2)}) collective-permute-start(bf16[2,8,2048]{2,1,0:T(8,128)(2,1)S(1)} %collective-permute-done.1), channel_id=1, source_target_pairs={{0,3},{1,4},{2,5},{3,6},{4,7},{5,8},{6,9},{7,10},{8,11},{9,12},{10... | collective-permute-start | bytes 196616 | tf_op jit(solution)/shard_map/ppermute | solution.py:24
  41.7 13.9 %collective-permute-start.5 = (bf16[3,2,8,2048]{3,2,1,0:T(8,128)(2,1)S(1)}, bf16[3,2,8,2048]{3,2,1,0:T(8,128)(2,1)S(1)}, u32[]{:S(2)}, u32[]{:S(2)}) collective-permute-start(bf16[3,2,8,2048]{3,2,1,0:T(8,128)(2,1)S(1)} %pad_maximum_fusion.p0), channel_id=1, source_target_pairs={{0,2},{1,3},{2,4},{3,5},{4,6},{5,7},{6,8},{7,9},{8,10},{9,11},{10,... | collective-permute-start | bytes 589832 | tf_op jit(solution)/shard_map/ppermute | solution.py:24
  48.3 10.3 %collective-permute-start.4 = (bf16[3,2,8,2048]{3,2,1,0:T(8,128)(2,1)S(1)}, bf16[3,2,8,2048]{3,2,1,0:T(8,128)(2,1)S(1)}, u32[]{:S(2)}, u32[]{:S(2)}) collective-permute-start(bf16[3,2,8,2048]{3,2,1,0:T(8,128)(2,1)S(1)} %pad_maximum_fusion.p0), channel_id=1, source_target_pairs={{0,15},{1,0},{2,1},{3,2},{4,3},{5,4},{6,5},{7,6},{8,7},{9,8},{10,9... | collective-permute-start | bytes 589832 | tf_op jit(solution)/shard_map/ppermute | solution.py:24
  52.3 9.2 %collective-permute-start.3 = (bf16[3,2,8,2048]{3,2,1,0:T(8,128)(2,1)S(1)}, bf16[3,2,8,2048]{3,2,1,0:T(8,128)(2,1)S(1)}, u32[]{:S(2)}, u32[]{:S(2)}) collective-permute-start(bf16[3,2,8,2048]{3,2,1,0:T(8,128)(2,1)S(1)} %pad_maximum_fusion.p0), channel_id=1, source_target_pairs={{0,1},{1,2},{2,3},{3,4},{4,5},{5,6},{6,7},{7,8},{8,9},{9,10},{10,1... | collective-permute-start | bytes 589832 | tf_op jit(solution)/shard_map/ppermute | solution.py:24
  64.6 15.7 %copy-start.2 = (f32[2048]{0:T(1024)S(1)}, f32[2048]{0:T(1024)}, u32[]{:S(2)}) copy-start(f32[2048]{0:T(1024)} %param.7) | copy-start | bytes 24580
  80.3 15.4 %copy-start.1 = (f32[8,2048]{1,0:T(8,128)}, f32[8,2048]{1,0:T(8,128)S(1)}, u32[]{:S(2)}) copy-start(f32[8,2048]{1,0:T(8,128)S(1)} %convert_reduce_fusion) | copy-start | bytes 196612
  95.8 16.7 %collective-permute-start.10 = (bf16[3,2,128,128]{3,2,1,0:T(8,128)(2,1)S(1)}, bf16[3,2,128,128]{3,2,1,0:T(8,128)(2,1)S(1)}, u32[]{:S(2)}, u32[]{:S(2)}) collective-permute-start(bf16[3,2,128,128]{3,2,1,0:T(8,128)(2,1)S(1)} %get-tuple-element.15), channel_id=1, source_target_pairs={{0,15},{1,0},{2,1},{3,2},{4,3},{5,4},{6,5},{7,6},{8,7},{9,8},{10,9... | collective-permute-start | bytes 589832 | tf_op jit(solution)/shard_map/ppermute | solution.py:24
  101.2 11.3 %collective-permute-start.11 = (bf16[3,2,128,128]{3,2,1,0:T(8,128)(2,1)S(1)}, bf16[3,2,128,128]{3,2,1,0:T(8,128)(2,1)S(1)}, u32[]{:S(2)}, u32[]{:S(2)}) collective-permute-start(bf16[3,2,128,128]{3,2,1,0:T(8,128)(2,1)S(1)} %get-tuple-element.16), channel_id=1, source_target_pairs={{0,1},{1,2},{2,3},{3,4},{4,5},{5,6},{6,7},{7,8},{8,9},{9,10},{10,1... | collective-permute-start | bytes 589832 | tf_op jit(solution)/shard_map/ppermute | solution.py:24
  103.1 11.3 %collective-permute-start.12 = (bf16[3,2,128,128]{3,2,1,0:T(8,128)(2,1)S(1)}, bf16[3,2,128,128]{3,2,1,0:T(8,128)(2,1)S(1)}, u32[]{:S(2)}, u32[]{:S(2)}) collective-permute-start(bf16[3,2,128,128]{3,2,1,0:T(8,128)(2,1)S(1)} %get-tuple-element.17), channel_id=1, source_target_pairs={{0,14},{1,15},{2,0},{3,1},{4,2},{5,3},{6,4},{7,5},{8,6},{9,7},{10,... | collective-permute-start | bytes 589832 | tf_op jit(solution)/shard_map/ppermute | solution.py:24
  106.2 13.9 %collective-permute-start.13 = (bf16[3,2,128,128]{3,2,1,0:T(8,128)(2,1)S(1)}, bf16[3,2,128,128]{3,2,1,0:T(8,128)(2,1)S(1)}, u32[]{:S(2)}, u32[]{:S(2)}) collective-permute-start(bf16[3,2,128,128]{3,2,1,0:T(8,128)(2,1)S(1)} %get-tuple-element.18), channel_id=1, source_target_pairs={{0,2},{1,3},{2,4},{3,5},{4,6},{5,7},{6,8},{7,9},{8,10},{9,11},{10,... | collective-permute-start | bytes 589832 | tf_op jit(solution)/shard_map/ppermute | solution.py:24
  110.5 13.2 %collective-permute-start.14 = (bf16[2,128,128]{2,1,0:T(8,128)(2,1)S(1)}, bf16[2,128,128]{2,1,0:T(8,128)(2,1)S(1)}, u32[]{:S(2)}, u32[]{:S(2)}) collective-permute-start(bf16[2,128,128]{2,1,0:T(8,128)(2,1)S(1)} %get-tuple-element.19), channel_id=1, source_target_pairs={{0,13},{1,14},{2,15},{3,0},{4,1},{5,2},{6,3},{7,4},{8,5},{9,6},{10... | collective-permute-start | bytes 196616 | tf_op jit(solution)/shard_map/ppermute | solution.py:24
  120.3 10.1 %collective-permute-start.16 = (bf16[2,128,128]{2,1,0:T(8,128)(2,1)S(1)}, bf16[2,128,128]{2,1,0:T(8,128)(2,1)S(1)}, u32[]{:S(2)}, u32[]{:S(2)}) collective-permute-start(bf16[2,128,128]{2,1,0:T(8,128)(2,1)S(1)} %fusion.4), channel_id=1, source_target_pairs={{0,5},{1,6},{2,7},{3,8},{4,9},{5,10},{6,11},{7,12},{8,13},{9,14},{... | collective-permute-start | bytes 196616 | tf_op jit(solution)/shard_map/ppermute | solution.py:24
  123.8 11.2 %collective-permute-start.15 = (bf16[2,128,128]{2,1,0:T(8,128)(2,1)S(1)}, bf16[2,128,128]{2,1,0:T(8,128)(2,1)S(1)}, u32[]{:S(2)}, u32[]{:S(2)}) collective-permute-start(bf16[2,128,128]{2,1,0:T(8,128)(2,1)S(1)} %fusion.1), channel_id=1, source_target_pairs={{0,11},{1,12},{2,13},{3,14},{4,15},{5,0},{6,1},{7,2},{8,3},{9,4},{... | collective-permute-start | bytes 196616 | tf_op jit(solution)/shard_map/ppermute | solution.py:24
  135.0 7.7 %collective-permute-start.17 = (f32[128,128]{1,0:T(8,128)S(1)}, f32[128,128]{1,0:T(8,128)S(1)}, u32[]{:S(2)}, u32[]{:S(2)}) collective-permute-start(f32[128,128]{1,0:T(8,128)S(1)} %slice_bitcast_fusion.2), channel_id=1, source_target_pairs={{0,16},{16,0},{1,17},{17,1},{2,18},{18,2},{3,19},{19,3},{4,20},{20... | collective-permute-start | bytes 196616 | tf_op jit(solution)/shard_map/ppermute | solution.py:154

commit v3 on v1

v3 whole, which is shorter than its diff:
```python
import functools

import jax
import jax.numpy as jnp
from jax import lax
from jax.experimental import pallas as pl
from jax.experimental.pallas import tpu as pltpu
from jax.sharding import Mesh
from jax.sharding import PartitionSpec as P

LINE = ("zh", "zl")
PAIR_LINE = ("c", "zh", "zl")
NT = (((1,), (1,)), ((), ()))
TN = (((0,), (0,)), ((), ()))
MAIN = 1920


def turned(x, steps):
    pairs = [
        (c * 16 + z, c * 16 + (z + (steps if c == 0 else -steps)) % 16)
        for c in range(2)
        for z in range(16)
    ]
    return lax.ppermute(x, PAIR_LINE, pairs)


def forward_kernel(core, ranks, main, rest, v, u, mine, theirs, coeffs):
    for j in range(4):
        if j < 3:
            x = main[:, pl.ds(j * 512, 512)]
        else:
            x = jnp.concatenate([main[:, pl.ds(1536, MAIN - 1536)], rest[...]], 1)
        tall = jnp.concatenate([v[i, j] for i in range(4)], 0)
        c = lax.dot_general(tall, x, NT, preferred_element_type=jnp.float32)
        for i in range(4):
            part = c[i * 80 : i * 80 + 80]
            level = lax.broadcasted_iota(jnp.int32, part.shape, 0)
            part = jnp.where(level < ranks[i, j], part, 0.0)
            coeffs[i, pl.ds(j * 80, 80), :] = part.astype(jnp.bfloat16)
    for i in range(4):
        tall = jnp.concatenate([u[i, j] for j in range(4)], 0)
        part = lax.dot_general(coeffs[i], tall, TN, preferred_element_type=jnp.float32)
        part = part.reshape(16, 2, 8, 512)
        first = core[0] == 0
        cols = pl.ds(i * 512, 512)
        mine[:, :, cols] = jnp.where(first, part[:, 0], part[:, 1])
        theirs[:, :, cols] = jnp.where(first, part[:, 1], part[:, 0]).astype(jnp.bfloat16)


def adjoint_kernel(at, w, v0, v1, u0, u1, own, one, two, three, coeffs, blocks):
    for k, u in enumerate((u0, u1)):
        for i in range(4):
            tall = jnp.concatenate([u[i, j] for j in range(4)], 0)
            a = lax.dot_general(tall, w[:, pl.ds(i * 512, 512)], NT, preferred_element_type=jnp.float32)
            for j in range(4):
                coeffs[k, j, pl.ds(i * 80, 80), :] = a[j * 80 : j * 80 + 80].astype(jnp.bfloat16)
    for k, v in enumerate((v0, v1)):
        side = jnp.bitwise_xor(at[0], k)
        for j in range(4):
            tall = jnp.concatenate([v[i, j] for i in range(4)], 0)
            back = lax.dot_general(coeffs[k, j], tall, TN, preferred_element_type=jnp.float32)
            back = back.astype(jnp.bfloat16)
            for q in range(4):
                blocks[q, side, j] = back[:, q * 128 : q * 128 + 128]
    own[...] = blocks[at[1]]
    one[...] = blocks[at[2]]
    two[...] = blocks[at[3]]
    three[...] = blocks[at[4]]


SMEM = pl.BlockSpec(memory_space=pltpu.SMEM)
VMEM = pl.BlockSpec(memory_space=pltpu.VMEM)
ROOM = pltpu.CompilerParams(vmem_limit_bytes=20 * 1024 * 1024)


def forward_part(core, ranks, main, rest, v, u):
    return pl.pallas_call(
        forward_kernel,
        out_shape=(
            jax.ShapeDtypeStruct((16, 8, 2048), jnp.float32),
            jax.ShapeDtypeStruct((16, 8, 2048), jnp.bfloat16),
        ),
        in_specs=[SMEM, SMEM] + [VMEM] * 4,
        out_specs=(VMEM, VMEM),
        scratch_shapes=[pltpu.VMEM((4, 320, 256), jnp.bfloat16)],
        compiler_params=ROOM,
        name="forward_part",
    )(core, ranks, main, rest, v, u)


def adjoint_part(at, weighted, v, u):
    blocks = jax.ShapeDtypeStruct((2, 4, 128, 128), jnp.bfloat16)
    return pl.pallas_call(
        adjoint_kernel,
        out_shape=(blocks,) * 4,
        in_specs=[SMEM] + [VMEM] * 5,
        out_specs=(VMEM,) * 4,
        scratch_shapes=[
            pltpu.VMEM((2, 4, 320, 128), jnp.bfloat16),
            pltpu.VMEM((4, 2, 4, 128, 128), jnp.bfloat16),
        ],
        compiler_params=ROOM,
        name="adjoint_part",
    )(at, weighted, *v, *u)


def exchange(blocks, axes):
    return lax.all_to_all(blocks, axes, split_axis=0, concat_axis=0, tiled=True)


def wide(x):
    return x.astype(jnp.float32)


def both_products(samples, row_weights, tile_ranks, u_factors, v_factors):
    core = lax.axis_index("c")
    place = lax.axis_index("zl")
    turn = 1 - 2 * core
    swap = functools.partial(lax.ppermute, axis_name="c", perm=[(0, 1), (1, 0)])

    x = samples.astype(jnp.bfloat16)
    rest = exchange(jnp.broadcast_to(x[:, MAIN:], (16, 16, 2048 - MAIN)), LINE).reshape(256, -1)
    main = lax.all_gather(x[:, :MAIN], LINE, axis=0, tiled=True)
    mine, theirs = forward_part(core[None].astype(jnp.int32), tile_ranks, main, rest, v_factors, u_factors)
    part = (mine + wide(swap(theirs))).astype(jnp.bfloat16)
    forward_rows = jnp.sum(wide(exchange(part, ("xy",))), axis=0)

    weighted = (forward_rows * row_weights[None, :]).astype(jnp.bfloat16)
    weighted, u_factors, v_factors = lax.optimization_barrier((weighted, u_factors, v_factors))
    weighted = exchange(jnp.broadcast_to(weighted, (16, 8, 2048)), ("xy",)).reshape(128, 2048)
    levels = lax.broadcasted_iota(jnp.int32, (1, 1, 80, 1), 2)
    ranked = jnp.where(levels < tile_ranks[:, :, None, None], u_factors, jnp.zeros_like(u_factors))
    v = (v_factors, swap(v_factors))
    u = (ranked, swap(ranked))

    at = jnp.stack([core, place, (place + turn) & 3, (place - turn) & 3, (place + 2) & 3]).astype(jnp.int32)
    own, one, two, three = adjoint_part(at, weighted, v, u)
    near = wide(own) + wide(turned(one, 1)) + wide(turned(two, -1)) + wide(turned(three, 2))
    near = near.astype(jnp.bfloat16).reshape(8, 128, 128)
    back = exchange(near, ("c", "zh")).reshape(2, 4, 16, 8, 128)
    back = jnp.sum(wide(back), axis=1)
    adjoint_cols = jnp.swapaxes(back, 0, 1).reshape(256, 128)
    return forward_rows, adjoint_cols


def solution(mesh):
    fine = Mesh(mesh.devices.reshape(16, 2, 4, 4), ("xy", "c", "zh", "zl"))
    narrow, wide_axes = LINE, ("xy", "c")
    in_specs = (
        P(narrow, wide_axes),
        P(narrow),
        P(narrow, wide_axes),
        P(narrow, wide_axes, None, None),
        P(narrow, wide_axes, None, None),
    )
    out_specs = (P(wide_axes, narrow), P(None, (*wide_axes, *narrow)))
    return jax.shard_map(both_products, mesh=fine, in_specs=in_specs, out_specs=out_specs, check_vma=False)
```

time: 149 us -> 155 us (1.040)
  blocking collectives: 44 us -> 59.3 us
  Pallas kernels: 10.1 us -> 5.4 us
  starting transfers between devices: 54.7 us -> 51 us
  waiting for transfers between devices: 27.8 us -> 30.7 us
  local copies, waits for them, and re-layouts: 5.75 us -> 3.59 us
    all_gather x0 -> x1, blocking collectives: none -> 29.6 us  [both_products(): main = lax.all_gather(x[:, :MAIN], LINE, axis=0, tiled=True)]
    all_to_all x2 -> x1, blocking collectives: 44 us -> 29.7 us  [exchange(): return lax.all_to_all(blocks, axes, split_axis=0, concat_axis=0, tiled=True)]
    ppermute x10 -> x6, starting transfers between devices: 34.5 us -> 24.9 us  [the longest x3 9.59 us: turned(): return lax.ppermute(x, PAIR_LINE, pairs)]
    all_to_all x2 -> x3, starting transfers between devices: 20.2 us -> 26.2 us  [exchange(): return lax.all_to_all(blocks, axes, split_axis=0, concat_axis=0, tiled=True)]
    pallas_call x2, Pallas kernels: 10.1 us -> 5.4 us  [the longest x1 3.63 us: adjoint_part(): pl.pallas_call(adjoint_kernel, out_shape=(blocks,) * 4, in_specs=[SMEM] +...]
    all_to_all x2 -> x3, waiting for transfers between devices: 18.4 us -> 20.6 us  [exchange(): return lax.all_to_all(blocks, axes, split_axis=0, concat_axis=0, tiled=True)]
    ppermute x10 -> x6, waiting for transfers between devices: 9.36 us -> 10.1 us  [the longest x3 8.56 us: turned(): return lax.ppermute(x, PAIR_LINE, pairs)]
  transfers between devices with their start and end apart: 12 -> 9, of which waited for: 5 -> 5; matrix products, arithmetic and copies ran while one was open for 3% -> 1% of each run, Pallas kernels for 0% -> 0%
where the time goes in v3:
time: 155 us; the launch traced here: 154 us
  blocking collectives  59.3 us (38%)
  starting transfers between devices  51 us (33%)
  waiting for transfers between devices  30.7 us (20%)
  Pallas kernels  5.4 us (3%)
  local copies, waits for them, and re-layouts  3.59 us (2%)
  other arithmetic  3.58 us (2%)
    all_to_all x1, blocking collectives, exchange(): return lax.all_to_all(blocks, axes, split_axis=0, concat_axis=0, tiled=True)  29.7 us
    all_gather x1, blocking collectives, both_products(): main = lax.all_gather(x[:, :MAIN], LINE, axis=0, tiled=True)  29.6 us
    all_to_all x3, starting transfers between devices, exchange(): return lax.all_to_all(blocks, axes, split_axis=0, concat_axis=0, tiled=True)  26.2 us
    all_to_all x3, waiting for transfers between devices, exchange(): return lax.all_to_all(blocks, axes, split_axis=0, concat_axis=0, tiled=True)  20.6 us
    ppermute x3, starting transfers between devices, turned(): return lax.ppermute(x, PAIR_LINE, pairs)  9.59 us
    ppermute x1, starting transfers between devices, both_products(): part = (mine + wide(swap(theirs))).astype(jnp.bfloat16)  9.38 us
    ppermute x3, waiting for transfers between devices, turned(): return lax.ppermute(x, PAIR_LINE, pairs)  8.56 us
    ppermute x1, starting transfers between devices, both_products(): u = (ranked, swap(ranked))  3.97 us
  transfers between devices with their start and end apart: 9, of which 5 were waited for; matrix products, arithmetic and copies ran while one was open for 1% of the time, Pallas kernels for 0%

profile of v3, /device:TPU:1, one launch (start us, length us, event | category | flops | bytes accessed | tf_op | source)
XLA Modules:
  0.0 154.4 jit_solution(9391027533872563912)
XLA Ops:
  0.6 1.0 convert_element_type.36
  2.3 15.7 %all-to-all-start = ((bf16[16,16,128]{2,1,0:T(8,128)(2,1)}), bf16[16,16,128]{2,1,0:T(8,128)(2,1)S(1)}, u32[]{:S(2)}, u32[]{:S(2)}) async-start(bf16[16,16,128]{2,1,0:T(8,128)(2,1)} %broadcast_in_dim.23), calls=%async_computation | async-start | bytes 131072 | tf_op jit(solution)/shard_map/all_to_all | solution.py:108
  18.1 29.6 %all_gather.3.main = bf16[256,1920]{1,0:T(8,128)(2,1)S(1)} all-gather(bf16[16,1920]{1,0:T(8,128)(2,1)S(1)} %slice.8), channel_id=1, replica_groups=mesh['xy'=16,'c'=2,'zh'=4,'zl'=4] {'zh','zl'}, dimensions={0}, use_global_device_ids=true | all-gather | bytes 1044480 | tf_op jit(solution)/shard_map/all_gather | solution.py:123
  47.7 1.3 copy-done.1
  49.0 1.8 %forward_part.1 = (f32[16,8,2048]{2,1,0:T(8,128)S(1)}, bf16[16,8,2048]{2,1,0:T(8,128)(2,1)S(1)}) custom-call(s32[1]{0:T(128)} %bitcast.core, s32[4,4]{1,0:T(4,128)S(1)} %copy-done.3, bf16[256,1920]{1,0:T(8,128)(2,1)S(1)} %all_gather.3.main, bf16[256,128]{1,0:T(8,128)(2,1)S(1)} %bitcast.13, bf16[4,4,80,512]{3,2,1,0:T(8,128)(2,1)S(1)} %copy-done.1, ...), custom_call_target="tpu_custom_call" | custom-call | tf_op jit(solution)/shard_map/forward_part/pallas_call | solution.py:77
  50.8 9.4 %collective-permute-start = (bf16[16,8,2048]{2,1,0:T(8,128)(2,1)S(1)}, bf16[16,8,2048]{2,1,0:T(8,128)(2,1)S(1)}, u32[]{:S(2)}, u32[]{:S(2)}) collective-permute-start(bf16[16,8,2048]{2,1,0:T(8,128)(2,1)S(1)} %get-tuple-element.12), channel_id=1, source_target_pairs={{0,16},{16,0},{1,17},{17,1},{2,18},{18,2},{3,19},{19,3},{4,20},{20... | collective-permute-start | bytes 1572872 | tf_op jit(solution)/shard_map/ppermute | solution.py:125
  60.2 1.5 collective-permute-done
  61.7 0.9 add_convert_fusion
  62.6 6.9 %all-to-all-start.1 = ((bf16[16,8,2048]{2,1,0:T(8,128)(2,1)}), bf16[16,8,2048]{2,1,0:T(8,128)(2,1)S(1)}, u32[]{:S(2)}, u32[]{:S(2)}) async-start(bf16[16,8,2048]{2,1,0:T(8,128)(2,1)} %add_convert_fusion), calls=%async_computation.1 | async-start | bytes 1048576 | tf_op jit(solution)/shard_map/all_to_all | solution.py:108
  69.6 10.3 %all-to-all-done.1 = bf16[16,8,2048]{2,1,0:T(8,128)(2,1)S(1)} async-done(((bf16[16,8,2048]{2,1,0:T(8,128)(2,1)}), bf16[16,8,2048]{2,1,0:T(8,128)(2,1)S(1)}, u32[]{:S(2)}, u32[]{:S(2)}) %all-to-all-start.1) | async-done | bytes 524320 | tf_op jit(solution)/shard_map/all_to_all | solution.py:108
  80.0 1.3 broadcast_select_fusion.u0
  81.3 4.0 %collective-permute-start.2 = (bf16[4,4,80,512]{3,2,1,0:T(8,128)(2,1)}, bf16[4,4,80,512]{3,2,1,0:T(8,128)(2,1)}, u32[]{:S(2)}, u32[]{:S(2)}) collective-permute-start(bf16[4,4,80,512]{3,2,1,0:T(8,128)(2,1)} %broadcast_select_fusion.u0), channel_id=1, source_target_pairs={{0,16},{16,0},{1,17},{17,1},{2,18},{18,2},{3,19},{19,3},{4,20},{20... | collective-permute-start | bytes 3932168 | tf_op jit(solution)/shard_map/ppermute | solution.py:134
  85.3 1.9 %collective-permute-start.1 = (bf16[4,4,80,512]{3,2,1,0:T(8,128)(2,1)S(1)}, bf16[4,4,80,512]{3,2,1,0:T(8,128)(2,1)}, u32[]{:S(2)}, u32[]{:S(2)}) collective-permute-start(bf16[4,4,80,512]{3,2,1,0:T(8,128)(2,1)S(1)} %copy-done.2), channel_id=1, source_target_pairs={{0,16},{16,0},{1,17},{17,1},{2,18},{18,2},{3,19},{19,3},{4,20},{20... | collective-permute-start | bytes 3932168 | tf_op jit(solution)/shard_map/ppermute | solution.py:133
  87.2 0.9 broadcast_in_dim.24
  88.1 3.6 %all-to-all-start.2 = ((bf16[16,8,2048]{2,1,0:T(8,128)(2,1)}), bf16[16,8,2048]{2,1,0:T(8,128)(2,1)S(1)}, u32[]{:S(2)}, u32[]{:S(2)}) async-start(bf16[16,8,2048]{2,1,0:T(8,128)(2,1)} %broadcast_in_dim.24), calls=%async_computation.2 | async-start | bytes 1048576 | tf_op jit(solution)/shard_map/all_to_all | solution.py:108
  91.7 10.3 %all-to-all-done.2 = bf16[16,8,2048]{2,1,0:T(8,128)(2,1)S(1)} async-done(((bf16[16,8,2048]{2,1,0:T(8,128)(2,1)}), bf16[16,8,2048]{2,1,0:T(8,128)(2,1)S(1)}, u32[]{:S(2)}, u32[]{:S(2)}) %all-to-all-start.2) | async-done | bytes 524320 | tf_op jit(solution)/shard_map/all_to_all | solution.py:108
  102.0 3.6 %adjoint_part.1 = (bf16[2,4,128,128]{3,2,1,0:T(8,128)(2,1)S(1)}, bf16[2,4,128,128]{3,2,1,0:T(8,128)(2,1)S(1)}, bf16[2,4,128,128]{3,2,1,0:T(8,128)(2,1)S(1)}, bf16[2,4,128,128]{3,2,1,0:T(8,128)(2,1)S(1)}) custom-call(s32[5]{0:T(128)S(1)} %stack.20.at, bf16[128,2048]{1,0:T(8,128)(2,1)S(1)} %bitcast.12, bf16[4,4,80,512]{3,2,1,0:T(8,128)(2,1)S(1)} %copy-done.2, ...), custom_call_target="tpu_custom_call" | custom-call | tf_op jit(solution)/shard_map/adjoint_part/pallas_call | solution.py:93
  105.7 2.9 %collective-permute-start.3 = (bf16[2,4,128,128]{3,2,1,0:T(8,128)(2,1)S(1)}, bf16[2,4,128,128]{3,2,1,0:T(8,128)(2,1)S(1)}, u32[]{:S(2)}, u32[]{:S(2)}) collective-permute-start(bf16[2,4,128,128]{3,2,1,0:T(8,128)(2,1)S(1)} %get-tuple-element.17), channel_id=1, source_target_pairs={{0,1},{1,2},{2,3},{3,4},{4,5},{5,6},{6,7},{7,8},{8,9},{9,10},{10,1... | collective-permute-start | bytes 786440 | tf_op jit(solution)/shard_map/ppermute | solution.py:24
  108.6 2.3 %collective-permute-start.4 = (bf16[2,4,128,128]{3,2,1,0:T(8,128)(2,1)S(1)}, bf16[2,4,128,128]{3,2,1,0:T(8,128)(2,1)S(1)}, u32[]{:S(2)}, u32[]{:S(2)}) collective-permute-start(bf16[2,4,128,128]{3,2,1,0:T(8,128)(2,1)S(1)} %get-tuple-element.18), channel_id=1, source_target_pairs={{0,15},{1,0},{2,1},{3,2},{4,3},{5,4},{6,5},{7,6},{8,7},{9,8},{10,9... | collective-permute-start | bytes 786440 | tf_op jit(solution)/shard_map/ppermute | solution.py:24
  111.0 4.3 %collective-permute-start.5 = (bf16[2,4,128,128]{3,2,1,0:T(8,128)(2,1)S(1)}, bf16[2,4,128,128]{3,2,1,0:T(8,128)(2,1)S(1)}, u32[]{:S(2)}, u32[]{:S(2)}) collective-permute-start(bf16[2,4,128,128]{3,2,1,0:T(8,128)(2,1)S(1)} %get-tuple-element.19), channel_id=1, source_target_pairs={{0,2},{1,3},{2,4},{3,5},{4,6},{5,7},{6,8},{7,9},{8,10},{9,11},{10,... | collective-permute-start | bytes 786440 | tf_op jit(solution)/shard_map/ppermute | solution.py:24
  115.3 4.2 %collective-permute-done.4 = bf16[2,4,128,128]{3,2,1,0:T(8,128)(2,1)S(1)} collective-permute-done((bf16[2,4,128,128]{3,2,1,0:T(8,128)(2,1)S(1)}, bf16[2,4,128,128]{3,2,1,0:T(8,128)(2,1)S(1)}, u32[]{:S(2)}, u32[]{:S(2)}) %collective-permute-start.4) | collective-permute-done | bytes 262176 | tf_op jit(solution)/shard_map/ppermute | solution.py:24
  119.5 4.4 %collective-permute-done.5 = bf16[2,4,128,128]{3,2,1,0:T(8,128)(2,1)S(1)} collective-permute-done((bf16[2,4,128,128]{3,2,1,0:T(8,128)(2,1)S(1)}, bf16[2,4,128,128]{3,2,1,0:T(8,128)(2,1)S(1)}, u32[]{:S(2)}, u32[]{:S(2)}) %collective-permute-start.5) | collective-permute-done | bytes 262176 | tf_op jit(solution)/shard_map/ppermute | solution.py:24
  124.0 29.7 %all_to_all.20 = bf16[8,128,128]{2,1,0:T(8,128)(2,1)S(1)} all-to-all(bf16[8,128,128]{2,1,0:T(8,128)(2,1)S(1)} %bitcast.14), channel_id=1, replica_groups=mesh['xy'=16,'c'=2,'zh'=4,'zl'=4] {'c','zh'}, dimensions={0} | all-to-all | bytes 524288 | tf_op jit(solution)/shard_map/all_to_all | solution.py:108
  153.8 0.7 copy.7
  (24 shorter events, 1.1 us)
Async XLA Ops:
  0.6 47.0 %copy-start = (bf16[4,4,80,512]{3,2,1,0:T(8,128)(2,1)S(1)}, bf16[4,4,80,512]{3,2,1,0:T(8,128)(2,1)}, u32[]{:S(2)}) copy-start(bf16[4,4,80,512]{3,2,1,0:T(8,128)(2,1)} %u.1) | copy-start | bytes 3932164
  0.6 47.0 %copy-start.3 = (s32[4,4]{1,0:T(4,128)S(1)}, s32[4,4]{1,0:T(4,128)}, u32[]{:S(2)}) copy-start(s32[4,4]{1,0:T(4,128)} %ranks.1) | copy-start | bytes 196
  2.3 45.3 %all-to-all-start = ((bf16[16,16,128]{2,1,0:T(8,128)(2,1)}), bf16[16,16,128]{2,1,0:T(8,128)(2,1)S(1)}, u32[]{:S(2)}, u32[]{:S(2)}) async-start(bf16[16,16,128]{2,1,0:T(8,128)(2,1)} %broadcast_in_dim.23), calls=%async_computation | async-start | bytes 131072 | tf_op jit(solution)/shard_map/all_to_all | solution.py:108
  47.7 1.3 copy-start.1
  50.8 10.9 %collective-permute-start = (bf16[16,8,2048]{2,1,0:T(8,128)(2,1)S(1)}, bf16[16,8,2048]{2,1,0:T(8,128)(2,1)S(1)}, u32[]{:S(2)}, u32[]{:S(2)}) collective-permute-start(bf16[16,8,2048]{2,1,0:T(8,128)(2,1)S(1)} %get-tuple-element.12), channel_id=1, source_target_pairs={{0,16},{16,0},{1,17},{17,1},{2,18},{18,2},{3,19},{19,3},{4,20},{20... | collective-permute-start | bytes 1572872 | tf_op jit(solution)/shard_map/ppermute | solution.py:125
  62.6 17.3 %copy-start.5 = (f32[2048]{0:T(1024)S(1)}, f32[2048]{0:T(1024)}, u32[]{:S(2)}) copy-start(f32[2048]{0:T(1024)} %param.6) | copy-start | bytes 24580
  62.6 17.3 %all-to-all-start.1 = ((bf16[16,8,2048]{2,1,0:T(8,128)(2,1)}), bf16[16,8,2048]{2,1,0:T(8,128)(2,1)S(1)}, u32[]{:S(2)}, u32[]{:S(2)}) async-start(bf16[16,8,2048]{2,1,0:T(8,128)(2,1)} %add_convert_fusion), calls=%async_computation.1 | async-start | bytes 1048576 | tf_op jit(solution)/shard_map/all_to_all | solution.py:108
  79.9 1.3 copy-start.4
  80.0 5.3 %copy-start.2 = (bf16[4,4,80,512]{3,2,1,0:T(8,128)(2,1)S(1)}, bf16[4,4,80,512]{3,2,1,0:T(8,128)(2,1)}, u32[]{:S(2)}) copy-start(bf16[4,4,80,512]{3,2,1,0:T(8,128)(2,1)} %v0) | copy-start | bytes 3932164
  81.3 20.7 %collective-permute-start.2 = (bf16[4,4,80,512]{3,2,1,0:T(8,128)(2,1)}, bf16[4,4,80,512]{3,2,1,0:T(8,128)(2,1)}, u32[]{:S(2)}, u32[]{:S(2)}) collective-permute-start(bf16[4,4,80,512]{3,2,1,0:T(8,128)(2,1)} %broadcast_select_fusion.u0), channel_id=1, source_target_pairs={{0,16},{16,0},{1,17},{17,1},{2,18},{18,2},{3,19},{19,3},{4,20},{20... | collective-permute-start | bytes 3932168 | tf_op jit(solution)/shard_map/ppermute | solution.py:134
  85.3 16.8 %collective-permute-start.1 = (bf16[4,4,80,512]{3,2,1,0:T(8,128)(2,1)S(1)}, bf16[4,4,80,512]{3,2,1,0:T(8,128)(2,1)}, u32[]{:S(2)}, u32[]{:S(2)}) collective-permute-start(bf16[4,4,80,512]{3,2,1,0:T(8,128)(2,1)S(1)} %copy-done.2), channel_id=1, source_target_pairs={{0,16},{16,0},{1,17},{17,1},{2,18},{18,2},{3,19},{19,3},{4,20},{20... | collective-permute-start | bytes 3932168 | tf_op jit(solution)/shard_map/ppermute | solution.py:133
  88.1 14.0 %all-to-all-start.2 = ((bf16[16,8,2048]{2,1,0:T(8,128)(2,1)}), bf16[16,8,2048]{2,1,0:T(8,128)(2,1)S(1)}, u32[]{:S(2)}, u32[]{:S(2)}) async-start(bf16[16,8,2048]{2,1,0:T(8,128)(2,1)} %broadcast_in_dim.24), calls=%async_computation.2 | async-start | bytes 1048576 | tf_op jit(solution)/shard_map/all_to_all | solution.py:108
  105.7 9.6 %collective-permute-start.3 = (bf16[2,4,128,128]{3,2,1,0:T(8,128)(2,1)S(1)}, bf16[2,4,128,128]{3,2,1,0:T(8,128)(2,1)S(1)}, u32[]{:S(2)}, u32[]{:S(2)}) collective-permute-start(bf16[2,4,128,128]{3,2,1,0:T(8,128)(2,1)S(1)} %get-tuple-element.17), channel_id=1, source_target_pairs={{0,1},{1,2},{2,3},{3,4},{4,5},{5,6},{6,7},{7,8},{8,9},{9,10},{10,1... | collective-permute-start | bytes 786440 | tf_op jit(solution)/shard_map/ppermute | solution.py:24
  108.6 10.9 %collective-permute-start.4 = (bf16[2,4,128,128]{3,2,1,0:T(8,128)(2,1)S(1)}, bf16[2,4,128,128]{3,2,1,0:T(8,128)(2,1)S(1)}, u32[]{:S(2)}, u32[]{:S(2)}) collective-permute-start(bf16[2,4,128,128]{3,2,1,0:T(8,128)(2,1)S(1)} %get-tuple-element.18), channel_id=1, source_target_pairs={{0,15},{1,0},{2,1},{3,2},{4,3},{5,4},{6,5},{7,6},{8,7},{9,8},{10,9... | collective-permute-start | bytes 786440 | tf_op jit(solution)/shard_map/ppermute | solution.py:24
  111.0 12.9 %collective-permute-start.5 = (bf16[2,4,128,128]{3,2,1,0:T(8,128)(2,1)S(1)}, bf16[2,4,128,128]{3,2,1,0:T(8,128)(2,1)S(1)}, u32[]{:S(2)}, u32[]{:S(2)}) collective-permute-start(bf16[2,4,128,128]{3,2,1,0:T(8,128)(2,1)S(1)} %get-tuple-element.19), channel_id=1, source_target_pairs={{0,2},{1,3},{2,4},{3,5},{4,6},{5,7},{6,8},{7,9},{8,10},{9,11},{10,... | collective-permute-start | bytes 786440 | tf_op jit(solution)/shard_map/ppermute | solution.py:24

commit v4 on v1

v4 whole, which is shorter than its diff:
```python
import functools

import jax
import jax.numpy as jnp
from jax import lax
from jax.experimental import pallas as pl
from jax.experimental.pallas import tpu as pltpu
from jax.sharding import Mesh
from jax.sharding import PartitionSpec as P

LINE = ("zh", "zl")
PAIR_LINE = ("c", "zh", "zl")
NT = (((1,), (1,)), ((), ()))
TN = (((0,), (0,)), ((), ()))


def turned(x, steps):
    pairs = [
        (c * 16 + z, c * 16 + (z + (steps if c == 0 else -steps)) % 16)
        for c in range(2)
        for z in range(16)
    ]
    return lax.ppermute(x, PAIR_LINE, pairs)


def forward_kernel(at, own, ahead, back, two, v0, v1, u0, u1, out, coeffs):
    for k, v in enumerate((v0, v1)):
        side = jnp.bitwise_xor(at[0], k)
        for j in range(4):
            cols = pl.ds(j * 512, 512)
            x = jnp.concatenate([piece[side, :, cols] for piece in (own, ahead, back, two)], 0)
            tall = jnp.concatenate([v[i, j] for i in range(4)], 0)
            c = lax.dot_general(tall, x, NT, preferred_element_type=jnp.float32)
            for i in range(4):
                coeffs[i, pl.ds(k * 320 + j * 80, 80), :] = c[i * 80 : i * 80 + 80].astype(jnp.bfloat16)
    for i in range(4):
        u = jnp.concatenate([u[i, j] for u in (u0, u1) for j in range(4)], 0)
        part = lax.dot_general(coeffs[i], u, TN, preferred_element_type=jnp.float32)
        for p in range(4):
            for zh in range(4):
                row = p * 32 + zh * 8
                out[zh * 4 + at[1 + p], :, pl.ds(i * 512, 512)] = part[row : row + 8].astype(jnp.bfloat16)


def adjoint_kernel(at, w, v0, v1, u0, u1, own, ahead, back, two, coeffs, blocks):
    for k, u in enumerate((u0, u1)):
        for i in range(4):
            tall = jnp.concatenate([u[i, j] for j in range(4)], 0)
            a = lax.dot_general(tall, w[:, pl.ds(i * 512, 512)], NT, preferred_element_type=jnp.float32)
            for j in range(4):
                coeffs[k, j, pl.ds(i * 80, 80), :] = a[j * 80 : j * 80 + 80].astype(jnp.bfloat16)
    for k, v in enumerate((v0, v1)):
        side = jnp.bitwise_xor(at[0], k)
        for j in range(4):
            tall = jnp.concatenate([v[i, j] for i in range(4)], 0)
            block = lax.dot_general(coeffs[k, j], tall, TN, preferred_element_type=jnp.float32)
            block = block.astype(jnp.bfloat16)
            for q in range(4):
                blocks[q, side, j] = block[:, q * 128 : q * 128 + 128]
    own[...] = blocks[at[1]]
    back[...] = blocks[at[2]]
    ahead[...] = blocks[at[3]]
    two[...] = blocks[at[4]]


SMEM = pl.BlockSpec(memory_space=pltpu.SMEM)
VMEM = pl.BlockSpec(memory_space=pltpu.VMEM)
ROOM = pltpu.CompilerParams(vmem_limit_bytes=20 * 1024 * 1024)


def forward_part(at, pieces, v, u):
    return pl.pallas_call(
        forward_kernel,
        out_shape=jax.ShapeDtypeStruct((16, 8, 2048), jnp.bfloat16),
        in_specs=[SMEM] + [VMEM] * 8,
        out_specs=VMEM,
        scratch_shapes=[pltpu.VMEM((4, 640, 128), jnp.bfloat16)],
        compiler_params=ROOM,
        name="forward_part",
    )(at, *pieces, *v, *u)


def adjoint_part(at, weighted, v, u):
    blocks = jax.ShapeDtypeStruct((2, 4, 128, 128), jnp.bfloat16)
    return pl.pallas_call(
        adjoint_kernel,
        out_shape=(blocks,) * 4,
        in_specs=[SMEM] + [VMEM] * 5,
        out_specs=(VMEM,) * 4,
        scratch_shapes=[
            pltpu.VMEM((2, 4, 320, 128), jnp.bfloat16),
            pltpu.VMEM((4, 2, 4, 128, 128), jnp.bfloat16),
        ],
        compiler_params=ROOM,
        name="adjoint_part",
    )(at, weighted, *v, *u)


def exchange(blocks, axes):
    return lax.all_to_all(blocks, axes, split_axis=0, concat_axis=0, tiled=True)


def wide(x):
    return x.astype(jnp.float32)


def both_products(samples, row_weights, tile_ranks, u_factors, v_factors):
    core = lax.axis_index("c")
    place = lax.axis_index("zl")
    turn = 1 - 2 * core
    swap = functools.partial(lax.ppermute, axis_name="c", perm=[(0, 1), (1, 0)])
    at = jnp.stack([core, place, (place - turn) & 3, (place + turn) & 3, (place + 2) & 3]).astype(jnp.int32)

    x = samples.astype(jnp.bfloat16).reshape(2, 1, 8, 2048)
    x = jnp.broadcast_to(x, (2, 4, 8, 2048)).reshape(8, 8, 2048)
    far = exchange(x, ("c", "zh")).reshape(2, 32, 2048)
    levels = lax.broadcasted_iota(jnp.int32, (1, 1, 80, 1), 2)
    ranked = jnp.where(levels < tile_ranks[:, :, None, None], u_factors, jnp.zeros_like(u_factors))
    v = (v_factors, swap(v_factors))
    u = (ranked, swap(ranked))

    two = turned(far, 2)
    ahead = turned(far, 1)
    back = turned(far, -1)
    part = forward_part(at, (far, ahead, back, two), v, u)
    forward_rows = jnp.sum(wide(exchange(part, ("xy",))), axis=0)

    weighted = (forward_rows * row_weights[None, :]).astype(jnp.bfloat16)
    weighted = exchange(jnp.broadcast_to(weighted, (16, 8, 2048)), ("xy",)).reshape(128, 2048)

    own, ahead, back, two = adjoint_part(at, weighted, v, u)
    two = turned(two, 2)
    ahead = turned(ahead, 1)
    back = turned(back, -1)
    near = wide(own) + wide(ahead) + wide(back) + wide(two)
    near = near.astype(jnp.bfloat16).reshape(8, 128, 128)
    blocks = exchange(near, ("c", "zh")).reshape(2, 4, 16, 8, 128)
    blocks = jnp.sum(wide(blocks), axis=1)
    adjoint_cols = jnp.swapaxes(blocks, 0, 1).reshape(256, 128)
    return forward_rows, adjoint_cols


def solution(mesh):
    fine = Mesh(mesh.devices.reshape(16, 2, 4, 4), ("xy", "c", "zh", "zl"))
    narrow, wide_axes = LINE, ("xy", "c")
    in_specs = (
        P(narrow, wide_axes),
        P(narrow),
        P(narrow, wide_axes),
        P(narrow, wide_axes, None, None),
        P(narrow, wide_axes, None, None),
    )
    out_specs = (P(wide_axes, narrow), P(None, (*wide_axes, *narrow)))
    return jax.shard_map(both_products, mesh=fine, in_specs=in_specs, out_specs=out_specs, check_vma=False)
```

time: 149 us -> 143 us (0.960)
  the two profiles are of different devices: /device:TPU:1 before, /device:TPU:33 now
where the time goes in v4:
time: 143 us
  blocking collectives  91.4 us (64%)
  starting transfers between devices  25.8 us (18%)
  waiting for transfers between devices  14.7 us (10%)
  Pallas kernels  6.43 us (4%)
  other arithmetic  2.69 us (2%)
    all_to_all x4, blocking collectives, exchange(): return lax.all_to_all(blocks, axes, split_axis=0, concat_axis=0, tiled=True)  91.4 us
    ppermute x6, starting transfers between devices, turned(): return lax.ppermute(x, PAIR_LINE, pairs)  21.3 us
    ppermute x6, waiting for transfers between devices, turned(): return lax.ppermute(x, PAIR_LINE, pairs)  14.7 us
    pallas_call x1, Pallas kernels, adjoint_part(): pl.pallas_call(adjoint_kernel, out_shape=(blocks,) * 4, in_specs=[SMEM] +...  3.25 us
    pallas_call x1, Pallas kernels, forward_part(): pl.pallas_call(forward_kernel, out_shape=jax.ShapeDtypeStruct((16, 8, 204...  3.18 us
  transfers between devices with their start and end apart: 8, of which 5 were waited for; matrix products, arithmetic and copies ran while one was open for 0% of the time, Pallas kernels for 0%

profile of v4, /device:TPU:33, one launch (start us, length us, event | category | flops | bytes accessed | tf_op | source)
XLA Modules:
  0.0 142.6 jit_solution(6843780503608562668)
XLA Ops:
  0.6 0.8 iota_compare_fusion
  1.4 1.7 %broadcast_select_fusion.u0 = bf16[4,4,80,512]{3,2,1,0:T(8,128)(2,1)S(1)} fusion(bf16[4,4,80,512]{3,2,1,0:T(8,128)(2,1)} %param.8, pred[4,4,80]{2,1,0:T(4,128)(4,1)S(1)} %iota_compare_fusion), kind=kLoop, calls=%fused_computation | loop fusion | flops 655360 | bytes 2622720 | tf_op jit(solution)/shard_map/jit(_where)/select_n | solution.py:118
  3.1 2.6 %collective-permute-start.4 = (bf16[4,4,80,512]{3,2,1,0:T(8,128)(2,1)S(1)}, bf16[4,4,80,512]{3,2,1,0:T(8,128)(2,1)}, u32[]{:S(2)}, u32[]{:S(2)}) collective-permute-start(bf16[4,4,80,512]{3,2,1,0:T(8,128)(2,1)S(1)} %broadcast_select_fusion.u0), channel_id=1, source_target_pairs={{0,16},{16,0},{1,17},{17,1},{2,18},{18,2},{3,19},{19,3},{4,20},{20... | collective-permute-start | bytes 3932168 | tf_op jit(solution)/shard_map/ppermute | solution.py:120
  5.7 1.9 %collective-permute-start.3 = (bf16[4,4,80,512]{3,2,1,0:T(8,128)(2,1)S(1)}, bf16[4,4,80,512]{3,2,1,0:T(8,128)(2,1)}, u32[]{:S(2)}, u32[]{:S(2)}) collective-permute-start(bf16[4,4,80,512]{3,2,1,0:T(8,128)(2,1)S(1)} %copy-done), channel_id=1, source_target_pairs={{0,16},{16,0},{1,17},{17,1},{2,18},{18,2},{3,19},{19,3},{4,20},{20... | collective-permute-start | bytes 3932168 | tf_op jit(solution)/shard_map/ppermute | solution.py:119
  7.7 35.5 %all_to_all.20 = bf16[8,8,2048]{2,1,0:T(8,128)(2,1)S(1)} all-to-all(bf16[8,8,2048]{2,1,0:T(8,128)(2,1)S(1)} %bitcast.21), channel_id=1, replica_groups=mesh['xy'=16,'c'=2,'zh'=4,'zl'=4] {'c','zh'}, dimensions={0} | all-to-all | bytes 524288 | tf_op jit(solution)/shard_map/all_to_all | solution.py:100
  43.2 1.9 %collective-permute-start.2 = (bf16[2,32,2048]{2,1,0:T(8,128)(2,1)S(1)}, bf16[2,32,2048]{2,1,0:T(8,128)(2,1)S(1)}, u32[]{:S(2)}, u32[]{:S(2)}) collective-permute-start(bf16[2,32,2048]{2,1,0:T(8,128)(2,1)S(1)} %bitcast.16), channel_id=1, source_target_pairs={{0,2},{1,3},{2,4},{3,5},{4,6},{5,7},{6,8},{7,9},{8,10},{9,11},{10,... | collective-permute-start | bytes 786440 | tf_op jit(solution)/shard_map/ppermute | solution.py:23
  45.1 2.3 %collective-permute-start.1 = (bf16[2,32,2048]{2,1,0:T(8,128)(2,1)S(1)}, bf16[2,32,2048]{2,1,0:T(8,128)(2,1)S(1)}, u32[]{:S(2)}, u32[]{:S(2)}) collective-permute-start(bf16[2,32,2048]{2,1,0:T(8,128)(2,1)S(1)} %bitcast.17), channel_id=1, source_target_pairs={{0,15},{1,0},{2,1},{3,2},{4,3},{5,4},{6,5},{7,6},{8,7},{9,8},{10,9... | collective-permute-start | bytes 786440 | tf_op jit(solution)/shard_map/ppermute | solution.py:23
  47.4 3.0 %collective-permute-start = (bf16[2,32,2048]{2,1,0:T(8,128)(2,1)S(1)}, bf16[2,32,2048]{2,1,0:T(8,128)(2,1)}, u32[]{:S(2)}, u32[]{:S(2)}) collective-permute-start(bf16[2,32,2048]{2,1,0:T(8,128)(2,1)S(1)} %bitcast.18), channel_id=1, source_target_pairs={{0,1},{1,2},{2,3},{3,4},{4,5},{5,6},{6,7},{7,8},{8,9},{9,10},{10,1... | collective-permute-start | bytes 786440 | tf_op jit(solution)/shard_map/ppermute | solution.py:23
  50.4 0.1 stack.23.at
  50.5 4.7 %collective-permute-done.2.two = bf16[2,32,2048]{2,1,0:T(8,128)(2,1)S(1)} collective-permute-done((bf16[2,32,2048]{2,1,0:T(8,128)(2,1)S(1)}, bf16[2,32,2048]{2,1,0:T(8,128)(2,1)S(1)}, u32[]{:S(2)}, u32[]{:S(2)}) %collective-permute-start.2) | collective-permute-done | bytes 262176 | tf_op jit(solution)/shard_map/ppermute | solution.py:23
  55.2 2.5 %collective-permute-done.1.back = bf16[2,32,2048]{2,1,0:T(8,128)(2,1)S(1)} collective-permute-done((bf16[2,32,2048]{2,1,0:T(8,128)(2,1)S(1)}, bf16[2,32,2048]{2,1,0:T(8,128)(2,1)S(1)}, u32[]{:S(2)}, u32[]{:S(2)}) %collective-permute-start.1) | collective-permute-done | bytes 262176 | tf_op jit(solution)/shard_map/ppermute | solution.py:23
  57.7 0.4 collective-permute-done.ahead
  58.1 3.2 %forward_part.1 = bf16[16,8,2048]{2,1,0:T(8,128)(2,1)S(1)} custom-call(s32[5]{0:T(128)S(1)} %stack.23.at, bf16[2,32,2048]{2,1,0:T(8,128)(2,1)S(1)} %bitcast.19, bf16[2,32,2048]{2,1,0:T(8,128)(2,1)} %collective-permute-done.ahead, bf16[2,32,2048]{2,1,0:T(8,128)(2,1)S(1)} %collective-permute-done.1.back, bf16[2,32,2048]{2,1,0:T(8,128)(2,1)S(1)} %collective-permute-done.2.two, ...), custom_call_target="tpu_custom_call" | custom-call | tf_op jit(solution)/shard_map/forward_part/pallas_call | solution.py:72
  61.3 15.5 %all_to_all.21 = bf16[16,8,2048]{2,1,0:T(8,128)(2,1)S(1)} all-to-all(bf16[16,8,2048]{2,1,0:T(8,128)(2,1)S(1)} %forward_part.1), channel_id=1, replica_groups=mesh['xy'=16,'c'=2,'zh'=4,'zl'=4] {'xy'}, dimensions={0} | all-to-all | bytes 1048576 | tf_op jit(solution)/shard_map/all_to_all | solution.py:100
  77.0 13.2 %all_to_all.22 = bf16[16,8,2048]{2,1,0:T(8,128)(2,1)S(1)} all-to-all(bf16[16,8,2048]{2,1,0:T(8,128)(2,1)S(1)} %broadcast_in_dim.27), channel_id=1, replica_groups=mesh['xy'=16,'c'=2,'zh'=4,'zl'=4] {'xy'}, dimensions={0} | all-to-all | bytes 1048576 | tf_op jit(solution)/shard_map/all_to_all | solution.py:100
  90.2 3.2 %adjoint_part.1 = (bf16[2,4,128,128]{3,2,1,0:T(8,128)(2,1)S(1)}, bf16[2,4,128,128]{3,2,1,0:T(8,128)(2,1)S(1)}, bf16[2,4,128,128]{3,2,1,0:T(8,128)(2,1)S(1)}, bf16[2,4,128,128]{3,2,1,0:T(8,128)(2,1)S(1)}) custom-call(s32[5]{0:T(128)S(1)} %stack.23.at, bf16[128,2048]{1,0:T(8,128)(2,1)S(1)} %bitcast.15, bf16[4,4,80,512]{3,2,1,0:T(8,128)(2,1)S(1)} %copy-done, ...), custom_call_target="tpu_custom_call" | custom-call | tf_op jit(solution)/shard_map/adjoint_part/pallas_call | solution.py:85
  93.5 3.5 %collective-permute-start.5 = (bf16[2,4,128,128]{3,2,1,0:T(8,128)(2,1)S(1)}, bf16[2,4,128,128]{3,2,1,0:T(8,128)(2,1)S(1)}, u32[]{:S(2)}, u32[]{:S(2)}) collective-permute-start(bf16[2,4,128,128]{3,2,1,0:T(8,128)(2,1)S(1)} %get-tuple-element.7), channel_id=1, source_target_pairs={{0,1},{1,2},{2,3},{3,4},{4,5},{5,6},{6,7},{7,8},{8,9},{9,10},{10,1... | collective-permute-start | bytes 786440 | tf_op jit(solution)/shard_map/ppermute | solution.py:23
  97.0 5.3 %collective-permute-start.6 = (bf16[2,4,128,128]{3,2,1,0:T(8,128)(2,1)S(1)}, bf16[2,4,128,128]{3,2,1,0:T(8,128)(2,1)S(1)}, u32[]{:S(2)}, u32[]{:S(2)}) collective-permute-start(bf16[2,4,128,128]{3,2,1,0:T(8,128)(2,1)S(1)} %get-tuple-element.8), channel_id=1, source_target_pairs={{0,15},{1,0},{2,1},{3,2},{4,3},{5,4},{6,5},{7,6},{8,7},{9,8},{10,9... | collective-permute-start | bytes 786440 | tf_op jit(solution)/shard_map/ppermute | solution.py:23
  102.4 5.3 %collective-permute-start.7 = (bf16[2,4,128,128]{3,2,1,0:T(8,128)(2,1)S(1)}, bf16[2,4,128,128]{3,2,1,0:T(8,128)(2,1)S(1)}, u32[]{:S(2)}, u32[]{:S(2)}) collective-permute-start(bf16[2,4,128,128]{3,2,1,0:T(8,128)(2,1)S(1)} %get-tuple-element.9), channel_id=1, source_target_pairs={{0,2},{1,3},{2,4},{3,5},{4,6},{5,7},{6,8},{7,9},{8,10},{9,11},{10,... | collective-permute-start | bytes 786440 | tf_op jit(solution)/shard_map/ppermute | solution.py:23
  107.6 0.2 collective-permute-done.6
  107.9 6.9 %collective-permute-done.7 = bf16[2,4,128,128]{3,2,1,0:T(8,128)(2,1)S(1)} collective-permute-done((bf16[2,4,128,128]{3,2,1,0:T(8,128)(2,1)S(1)}, bf16[2,4,128,128]{3,2,1,0:T(8,128)(2,1)S(1)}, u32[]{:S(2)}, u32[]{:S(2)}) %collective-permute-start.7) | collective-permute-done | bytes 262176 | tf_op jit(solution)/shard_map/ppermute | solution.py:23
  114.7 0.1 add_convert_fusion
  114.9 27.1 %all_to_all.23 = bf16[8,128,128]{2,1,0:T(8,128)(2,1)S(1)} all-to-all(bf16[8,128,128]{2,1,0:T(8,128)(2,1)S(1)} %bitcast.20), channel_id=1, replica_groups=mesh['xy'=16,'c'=2,'zh'=4,'zl'=4] {'c','zh'}, dimensions={0} | all-to-all | bytes 524288 | tf_op jit(solution)/shard_map/all_to_all | solution.py:100
  142.0 0.7 copy.7
  (17 shorter events, 0.2 us)
Async XLA Ops:
  1.4 4.3 %copy-start = (bf16[4,4,80,512]{3,2,1,0:T(8,128)(2,1)S(1)}, bf16[4,4,80,512]{3,2,1,0:T(8,128)(2,1)}, u32[]{:S(2)}) copy-start(bf16[4,4,80,512]{3,2,1,0:T(8,128)(2,1)} %v0.3) | copy-start | bytes 3932164
  1.4 6.2 %copy-start.2 = (f32[16,2048]{1,0:T(8,128)S(1)}, f32[16,2048]{1,0:T(8,128)}, u32[]{:S(2)}) copy-start(f32[16,2048]{1,0:T(8,128)} %param.5) | copy-start | bytes 393220
  3.1 55.0 %collective-permute-start.4 = (bf16[4,4,80,512]{3,2,1,0:T(8,128)(2,1)S(1)}, bf16[4,4,80,512]{3,2,1,0:T(8,128)(2,1)}, u32[]{:S(2)}, u32[]{:S(2)}) collective-permute-start(bf16[4,4,80,512]{3,2,1,0:T(8,128)(2,1)S(1)} %broadcast_select_fusion.u0), channel_id=1, source_target_pairs={{0,16},{16,0},{1,17},{17,1},{2,18},{18,2},{3,19},{19,3},{4,20},{20... | collective-permute-start | bytes 3932168 | tf_op jit(solution)/shard_map/ppermute | solution.py:120
  5.7 52.4 %collective-permute-start.3 = (bf16[4,4,80,512]{3,2,1,0:T(8,128)(2,1)S(1)}, bf16[4,4,80,512]{3,2,1,0:T(8,128)(2,1)}, u32[]{:S(2)}, u32[]{:S(2)}) collective-permute-start(bf16[4,4,80,512]{3,2,1,0:T(8,128)(2,1)S(1)} %copy-done), channel_id=1, source_target_pairs={{0,16},{16,0},{1,17},{17,1},{2,18},{18,2},{3,19},{19,3},{4,20},{20... | collective-permute-start | bytes 3932168 | tf_op jit(solution)/shard_map/ppermute | solution.py:119
  43.2 12.0 %collective-permute-start.2 = (bf16[2,32,2048]{2,1,0:T(8,128)(2,1)S(1)}, bf16[2,32,2048]{2,1,0:T(8,128)(2,1)S(1)}, u32[]{:S(2)}, u32[]{:S(2)}) collective-permute-start(bf16[2,32,2048]{2,1,0:T(8,128)(2,1)S(1)} %bitcast.16), channel_id=1, source_target_pairs={{0,2},{1,3},{2,4},{3,5},{4,6},{5,7},{6,8},{7,9},{8,10},{9,11},{10,... | collective-permute-start | bytes 786440 | tf_op jit(solution)/shard_map/ppermute | solution.py:23
  45.1 12.6 %collective-permute-start.1 = (bf16[2,32,2048]{2,1,0:T(8,128)(2,1)S(1)}, bf16[2,32,2048]{2,1,0:T(8,128)(2,1)S(1)}, u32[]{:S(2)}, u32[]{:S(2)}) collective-permute-start(bf16[2,32,2048]{2,1,0:T(8,128)(2,1)S(1)} %bitcast.17), channel_id=1, source_target_pairs={{0,15},{1,0},{2,1},{3,2},{4,3},{5,4},{6,5},{7,6},{8,7},{9,8},{10,9... | collective-permute-start | bytes 786440 | tf_op jit(solution)/shard_map/ppermute | solution.py:23
  47.4 10.7 %collective-permute-start = (bf16[2,32,2048]{2,1,0:T(8,128)(2,1)S(1)}, bf16[2,32,2048]{2,1,0:T(8,128)(2,1)}, u32[]{:S(2)}, u32[]{:S(2)}) collective-permute-start(bf16[2,32,2048]{2,1,0:T(8,128)(2,1)S(1)} %bitcast.18), channel_id=1, source_target_pairs={{0,1},{1,2},{2,3},{3,4},{4,5},{5,6},{6,7},{7,8},{8,9},{9,10},{10,1... | collective-permute-start | bytes 786440 | tf_op jit(solution)/shard_map/ppermute | solution.py:23
  61.2 15.6 %copy-start.3 = (f32[2048]{0:T(1024)S(1)}, f32[2048]{0:T(1024)}, u32[]{:S(2)}) copy-start(f32[2048]{0:T(1024)} %param.6) | copy-start | bytes 24580
  76.9 16.6 %copy-start.1 = (f32[8,2048]{1,0:T(8,128)}, f32[8,2048]{1,0:T(8,128)S(1)}, u32[]{:S(2)}) copy-start(f32[8,2048]{1,0:T(8,128)S(1)} %convert_reduce_fusion) | copy-start | bytes 196612
  93.5 14.1 %collective-permute-start.5 = (bf16[2,4,128,128]{3,2,1,0:T(8,128)(2,1)S(1)}, bf16[2,4,128,128]{3,2,1,0:T(8,128)(2,1)S(1)}, u32[]{:S(2)}, u32[]{:S(2)}) collective-permute-start(bf16[2,4,128,128]{3,2,1,0:T(8,128)(2,1)S(1)} %get-tuple-element.7), channel_id=1, source_target_pairs={{0,1},{1,2},{2,3},{3,4},{4,5},{5,6},{6,7},{7,8},{8,9},{9,10},{10,1... | collective-permute-start | bytes 786440 | tf_op jit(solution)/shard_map/ppermute | solution.py:23
  97.0 10.8 %collective-permute-start.6 = (bf16[2,4,128,128]{3,2,1,0:T(8,128)(2,1)S(1)}, bf16[2,4,128,128]{3,2,1,0:T(8,128)(2,1)S(1)}, u32[]{:S(2)}, u32[]{:S(2)}) collective-permute-start(bf16[2,4,128,128]{3,2,1,0:T(8,128)(2,1)S(1)} %get-tuple-element.8), channel_id=1, source_target_pairs={{0,15},{1,0},{2,1},{3,2},{4,3},{5,4},{6,5},{7,6},{8,7},{9,8},{10,9... | collective-permute-start | bytes 786440 | tf_op jit(solution)/shard_map/ppermute | solution.py:23
  102.4 12.3 %collective-permute-start.7 = (bf16[2,4,128,128]{3,2,1,0:T(8,128)(2,1)S(1)}, bf16[2,4,128,128]{3,2,1,0:T(8,128)(2,1)S(1)}, u32[]{:S(2)}, u32[]{:S(2)}) collective-permute-start(bf16[2,4,128,128]{3,2,1,0:T(8,128)(2,1)S(1)} %get-tuple-element.9), channel_id=1, source_target_pairs={{0,2},{1,3},{2,4},{3,5},{4,6},{5,7},{6,8},{7,9},{8,10},{9,11},{10,... | collective-permute-start | bytes 786440 | tf_op jit(solution)/shard_map/ppermute | solution.py:23

commit v5 on v4

--- a/solution.py
+++ b/solution.py
@@ -23,16 +23,18 @@
     return lax.ppermute(x, PAIR_LINE, pairs)
 
 
-def forward_kernel(at, own, ahead, back, two, v0, v1, u0, u1, out, coeffs):
+def coeffs_kernel(own, ahead, back, two, v0, v1, coeffs):
     for k, v in enumerate((v0, v1)):
-        side = jnp.bitwise_xor(at[0], k)
         for j in range(4):
-            cols = pl.ds(j * 512, 512)
-            x = jnp.concatenate([piece[side, :, cols] for piece in (own, ahead, back, two)], 0)
+            cols = pl.ds(k * 2048 + j * 512, 512)
+            x = jnp.concatenate([piece[:, cols] for piece in (own, ahead, back, two)], 0)
             tall = jnp.concatenate([v[i, j] for i in range(4)], 0)
             c = lax.dot_general(tall, x, NT, preferred_element_type=jnp.float32)
             for i in range(4):
                 coeffs[i, pl.ds(k * 320 + j * 80, 80), :] = c[i * 80 : i * 80 + 80].astype(jnp.bfloat16)
+
+
+def forward_kernel(at, coeffs, u0, u1, out):
     for i in range(4):
         u = jnp.concatenate([u[i, j] for u in (u0, u1) for j in range(4)], 0)
         part = lax.dot_general(coeffs[i], u, TN, preferred_element_type=jnp.float32)
@@ -69,15 +71,22 @@
 
 
 def forward_part(at, pieces, v, u):
+    coeffs = pl.pallas_call(
+        coeffs_kernel,
+        out_shape=jax.ShapeDtypeStruct((4, 640, 128), jnp.bfloat16),
+        in_specs=[VMEM] * 6,
+        out_specs=VMEM,
+        compiler_params=ROOM,
+        name="forward_coeffs",
+    )(*pieces, *v)
     return pl.pallas_call(
         forward_kernel,
         out_shape=jax.ShapeDtypeStruct((16, 8, 2048), jnp.bfloat16),
-        in_specs=[SMEM] + [VMEM] * 8,
+        in_specs=[SMEM] + [VMEM] * 3,
         out_specs=VMEM,
-        scratch_shapes=[pltpu.VMEM((4, 640, 128), jnp.bfloat16)],
         compiler_params=ROOM,
         name="forward_part",
-    )(at, *pieces, *v, *u)
+    )(at, coeffs, *u)
 
 
 def adjoint_part(at, weighted, v, u):
@@ -111,17 +120,19 @@
     swap = functools.partial(lax.ppermute, axis_name="c", perm=[(0, 1), (1, 0)])
     at = jnp.stack([core, place, (place - turn) & 3, (place + turn) & 3, (place + 2) & 3]).astype(jnp.int32)
 
-    x = samples.astype(jnp.bfloat16).reshape(2, 1, 8, 2048)
-    x = jnp.broadcast_to(x, (2, 4, 8, 2048)).reshape(8, 8, 2048)
-    far = exchange(x, ("c", "zh")).reshape(2, 32, 2048)
+    x = samples.astype(jnp.bfloat16).reshape(2, 8, 2048)
+    kept = lax.dynamic_index_in_dim(x, core, 0, keepdims=False)
+    given = lax.dynamic_index_in_dim(x, 1 - core, 0, keepdims=False)
+    block = jnp.concatenate([kept, swap(given)], 1)
+    far = lax.all_gather(block, "zh", axis=0, tiled=True)
+    far, u_factors, v_factors = lax.optimization_barrier((far, u_factors, v_factors))
+    two = turned(far, 2)
+    ahead = turned(far, 1)
+    back = turned(far, -1)
     levels = lax.broadcasted_iota(jnp.int32, (1, 1, 80, 1), 2)
     ranked = jnp.where(levels < tile_ranks[:, :, None, None], u_factors, jnp.zeros_like(u_factors))
     v = (v_factors, swap(v_factors))
     u = (ranked, swap(ranked))
-
-    two = turned(far, 2)
-    ahead = turned(far, 1)
-    back = turned(far, -1)
     part = forward_part(at, (far, ahead, back, two), v, u)
     forward_rows = jnp.sum(wide(exchange(part, ("xy",))), axis=0)
 

time: 143 us -> 144 us (level)
  the two profiles are of different devices: /device:TPU:33 before, /device:TPU:1 now
where the time goes in v5:
time: 144 us; the launch traced here: 143 us
  blocking collectives  75.1 us (52%)
  starting transfers between devices  39.1 us (27%)
  waiting for transfers between devices  16 us (11%)
  Pallas kernels  7.43 us (5%)
  other arithmetic  3.49 us (2%)
    all_to_all x3, blocking collectives, exchange(): return lax.all_to_all(blocks, axes, split_axis=0, concat_axis=0, tiled=True)  56 us
    ppermute x6, starting transfers between devices, turned(): return lax.ppermute(x, PAIR_LINE, pairs)  22.7 us
    all_gather x1, blocking collectives, both_products(): far = lax.all_gather(block, 'zh', axis=0, tiled=True)  19.2 us
    ppermute x6, waiting for transfers between devices, turned(): return lax.ppermute(x, PAIR_LINE, pairs)  16 us
    ppermute x1, starting transfers between devices, both_products(): block = jnp.concatenate([kept, swap(given)], 1)  8.75 us
    ppermute x1, starting transfers between devices, both_products(): v = (v_factors, swap(v_factors))  5.74 us
    pallas_call x1, Pallas kernels, adjoint_part(): pl.pallas_call(adjoint_kernel, out_shape=(blocks,) * 4, in_specs=[SMEM] +...  3.25 us
  transfers between devices with their start and end apart: 9, of which 5 were waited for; matrix products, arithmetic and copies ran while one was open for 2% of the time, Pallas kernels for 2%

profile of v5, /device:TPU:1, one launch (start us, length us, event | category | flops | bytes accessed | tf_op | source)
XLA Modules:
  0.0 142.8 jit_solution(8791540260431327541)
XLA Ops:
  0.6 0.9 convert_bitcast_fusion
  1.6 8.7 %collective-permute-start = (bf16[8,2048]{1,0:T(8,128)(2,1)S(1)}, bf16[8,2048]{1,0:T(8,128)(2,1)S(1)}, u32[]{:S(2)}, u32[]{:S(2)}) collective-permute-start(bf16[8,2048]{1,0:T(8,128)(2,1)S(1)} %get-tuple-element.17), channel_id=1, source_target_pairs={{0,16},{16,0},{1,17},{17,1},{2,18},{18,2},{3,19},{19,3},{4,20},{20... | collective-permute-start | bytes 98312 | tf_op jit(solution)/shard_map/ppermute | solution.py:126
  10.3 0.8 iota_compare_fusion
  11.2 19.2 %all_gather.3.own = bf16[32,4096]{1,0:T(8,128)(2,1)S(1)} all-gather(bf16[8,4096]{1,0:T(8,128)(2,1)S(1)} %pad_maximum_fusion), channel_id=1, replica_groups=mesh['xy'=16,'c'=2,'zh'=4,'zl'=4] {'zh'}, dimensions={0}, use_global_device_ids=true | all-gather | bytes 327680 | tf_op jit(solution)/shard_map/all_gather | solution.py:127
  30.3 5.7 %collective-permute-start.4 = (bf16[4,4,80,512]{3,2,1,0:T(8,128)(2,1)}, bf16[4,4,80,512]{3,2,1,0:T(8,128)(2,1)}, u32[]{:S(2)}, u32[]{:S(2)}) collective-permute-start(bf16[4,4,80,512]{3,2,1,0:T(8,128)(2,1)} %v0.1), channel_id=1, source_target_pairs={{0,16},{16,0},{1,17},{17,1},{2,18},{18,2},{3,19},{19,3},{4,20},{20... | collective-permute-start | bytes 3932168 | tf_op jit(solution)/shard_map/ppermute | solution.py:134
  36.1 1.6 %broadcast_select_fusion.u0 = bf16[4,4,80,512]{3,2,1,0:T(8,128)(2,1)S(1)} fusion(bf16[4,4,80,512]{3,2,1,0:T(8,128)(2,1)} %param.8, pred[4,4,80]{2,1,0:T(4,128)(4,1)S(1)} %iota_compare_fusion), kind=kLoop, calls=%fused_computation | loop fusion | flops 655360 | bytes 2622720 | tf_op jit(solution)/shard_map/jit(_where)/select_n | solution.py:133
  37.6 1.9 %collective-permute-start.5 = (bf16[4,4,80,512]{3,2,1,0:T(8,128)(2,1)S(1)}, bf16[4,4,80,512]{3,2,1,0:T(8,128)(2,1)}, u32[]{:S(2)}, u32[]{:S(2)}) collective-permute-start(bf16[4,4,80,512]{3,2,1,0:T(8,128)(2,1)S(1)} %broadcast_select_fusion.u0), channel_id=1, source_target_pairs={{0,16},{16,0},{1,17},{17,1},{2,18},{18,2},{3,19},{19,3},{4,20},{20... | collective-permute-start | bytes 3932168 | tf_op jit(solution)/shard_map/ppermute | solution.py:135
  39.5 3.3 %collective-permute-start.1 = (bf16[32,4096]{1,0:T(8,128)(2,1)S(1)}, bf16[32,4096]{1,0:T(8,128)(2,1)S(1)}, u32[]{:S(2)}, u32[]{:S(2)}) collective-permute-start(bf16[32,4096]{1,0:T(8,128)(2,1)S(1)} %all_gather.3.own), channel_id=1, source_target_pairs={{0,1},{1,2},{2,3},{3,4},{4,5},{5,6},{6,7},{7,8},{8,9},{9,10},{10,1... | collective-permute-start | bytes 786440 | tf_op jit(solution)/shard_map/ppermute | solution.py:23
  42.8 2.0 %collective-permute-start.2 = (bf16[32,4096]{1,0:T(8,128)(2,1)S(1)}, bf16[32,4096]{1,0:T(8,128)(2,1)S(1)}, u32[]{:S(2)}, u32[]{:S(2)}) collective-permute-start(bf16[32,4096]{1,0:T(8,128)(2,1)S(1)} %all_gather.3.own), channel_id=1, source_target_pairs={{0,15},{1,0},{2,1},{3,2},{4,3},{5,4},{6,5},{7,6},{8,7},{9,8},{10,9... | collective-permute-start | bytes 786440 | tf_op jit(solution)/shard_map/ppermute | solution.py:23
  44.8 3.0 %collective-permute-start.3 = (bf16[32,4096]{1,0:T(8,128)(2,1)S(1)}, bf16[32,4096]{1,0:T(8,128)(2,1)}, u32[]{:S(2)}, u32[]{:S(2)}) collective-permute-start(bf16[32,4096]{1,0:T(8,128)(2,1)S(1)} %all_gather.3.own), channel_id=1, source_target_pairs={{0,2},{1,3},{2,4},{3,5},{4,6},{5,7},{6,8},{7,9},{8,10},{9,11},{10,... | collective-permute-start | bytes 786440 | tf_op jit(solution)/shard_map/ppermute | solution.py:23
  48.0 3.7 %collective-permute-done.2.back = bf16[32,4096]{1,0:T(8,128)(2,1)S(1)} collective-permute-done((bf16[32,4096]{1,0:T(8,128)(2,1)S(1)}, bf16[32,4096]{1,0:T(8,128)(2,1)S(1)}, u32[]{:S(2)}, u32[]{:S(2)}) %collective-permute-start.2) | collective-permute-done | bytes 262176 | tf_op jit(solution)/shard_map/ppermute | solution.py:23
  51.6 5.6 %collective-permute-done.3.two = bf16[32,4096]{1,0:T(8,128)(2,1)} collective-permute-done((bf16[32,4096]{1,0:T(8,128)(2,1)S(1)}, bf16[32,4096]{1,0:T(8,128)(2,1)}, u32[]{:S(2)}, u32[]{:S(2)}) %collective-permute-start.3) | collective-permute-done | bytes 262176 | tf_op jit(solution)/shard_map/ppermute | solution.py:23
  57.2 2.2 %forward_coeffs.1.coeffs = bf16[4,640,128]{2,1,0:T(8,128)(2,1)S(1)} custom-call(bf16[32,4096]{1,0:T(8,128)(2,1)S(1)} %all_gather.3.own, bf16[32,4096]{1,0:T(8,128)(2,1)S(1)} %collective-permute-done.1.ahead, bf16[32,4096]{1,0:T(8,128)(2,1)S(1)} %collective-permute-done.2.back, bf16[32,4096]{1,0:T(8,128)(2,1)} %collective-permute-done.3.two, ...), custom_call_target="tpu_custom_call" | custom-call | tf_op jit(solution)/shard_map/forward_coeffs/pallas_call | solution.py:74
  59.5 1.9 %forward_part.1 = bf16[16,8,2048]{2,1,0:T(8,128)(2,1)S(1)} custom-call(s32[5]{0:T(128)S(1)} %stack.23.at, bf16[4,640,128]{2,1,0:T(8,128)(2,1)S(1)} %forward_coeffs.1.coeffs, bf16[4,4,80,512]{3,2,1,0:T(8,128)(2,1)S(1)} %broadcast_select_fusion.u0, bf16[4,4,80,512]{3,2,1,0:T(8,128)(2,1)} %collective-permute-done.5.u1), custom_call_target="tpu_custom_call" | custom-call | tf_op jit(solution)/shard_map/forward_part/pallas_call | solution.py:82
  61.4 15.5 %all_to_all.15 = bf16[16,8,2048]{2,1,0:T(8,128)(2,1)S(1)} all-to-all(bf16[16,8,2048]{2,1,0:T(8,128)(2,1)S(1)} %forward_part.1), channel_id=1, replica_groups=mesh['xy'=16,'c'=2,'zh'=4,'zl'=4] {'xy'}, dimensions={0} | all-to-all | bytes 1048576 | tf_op jit(solution)/shard_map/all_to_all | solution.py:109
  77.1 12.2 %all_to_all.16 = bf16[16,8,2048]{2,1,0:T(8,128)(2,1)S(1)} all-to-all(bf16[16,8,2048]{2,1,0:T(8,128)(2,1)S(1)} %broadcast_in_dim.18), channel_id=1, replica_groups=mesh['xy'=16,'c'=2,'zh'=4,'zl'=4] {'xy'}, dimensions={0} | all-to-all | bytes 1048576 | tf_op jit(solution)/shard_map/all_to_all | solution.py:109
  89.3 3.2 %adjoint_part.1 = (bf16[2,4,128,128]{3,2,1,0:T(8,128)(2,1)S(1)}, bf16[2,4,128,128]{3,2,1,0:T(8,128)(2,1)S(1)}, bf16[2,4,128,128]{3,2,1,0:T(8,128)(2,1)S(1)}, bf16[2,4,128,128]{3,2,1,0:T(8,128)(2,1)S(1)}) custom-call(s32[5]{0:T(128)S(1)} %stack.23.at, bf16[128,2048]{1,0:T(8,128)(2,1)S(1)} %bitcast.17, bf16[4,4,80,512]{3,2,1,0:T(8,128)(2,1)S(1)} %copy-done, ...), custom_call_target="tpu_custom_call" | custom-call | tf_op jit(solution)/shard_map/adjoint_part/pallas_call | solution.py:94
  92.6 2.4 %collective-permute-start.6 = (bf16[2,4,128,128]{3,2,1,0:T(8,128)(2,1)S(1)}, bf16[2,4,128,128]{3,2,1,0:T(8,128)(2,1)S(1)}, u32[]{:S(2)}, u32[]{:S(2)}) collective-permute-start(bf16[2,4,128,128]{3,2,1,0:T(8,128)(2,1)S(1)} %get-tuple-element.13), channel_id=1, source_target_pairs={{0,1},{1,2},{2,3},{3,4},{4,5},{5,6},{6,7},{7,8},{8,9},{9,10},{10,1... | collective-permute-start | bytes 786440 | tf_op jit(solution)/shard_map/ppermute | solution.py:23
  95.0 2.9 %collective-permute-start.7 = (bf16[2,4,128,128]{3,2,1,0:T(8,128)(2,1)S(1)}, bf16[2,4,128,128]{3,2,1,0:T(8,128)(2,1)S(1)}, u32[]{:S(2)}, u32[]{:S(2)}) collective-permute-start(bf16[2,4,128,128]{3,2,1,0:T(8,128)(2,1)S(1)} %get-tuple-element.14), channel_id=1, source_target_pairs={{0,15},{1,0},{2,1},{3,2},{4,3},{5,4},{6,5},{7,6},{8,7},{9,8},{10,9... | collective-permute-start | bytes 786440 | tf_op jit(solution)/shard_map/ppermute | solution.py:23
  97.9 9.1 %collective-permute-start.8 = (bf16[2,4,128,128]{3,2,1,0:T(8,128)(2,1)S(1)}, bf16[2,4,128,128]{3,2,1,0:T(8,128)(2,1)S(1)}, u32[]{:S(2)}, u32[]{:S(2)}) collective-permute-start(bf16[2,4,128,128]{3,2,1,0:T(8,128)(2,1)S(1)} %get-tuple-element.15), channel_id=1, source_target_pairs={{0,2},{1,3},{2,4},{3,5},{4,6},{5,7},{6,8},{7,9},{8,10},{9,11},{10,... | collective-permute-start | bytes 786440 | tf_op jit(solution)/shard_map/ppermute | solution.py:23
  107.0 2.6 %collective-permute-done.7 = bf16[2,4,128,128]{3,2,1,0:T(8,128)(2,1)S(1)} collective-permute-done((bf16[2,4,128,128]{3,2,1,0:T(8,128)(2,1)S(1)}, bf16[2,4,128,128]{3,2,1,0:T(8,128)(2,1)S(1)}, u32[]{:S(2)}, u32[]{:S(2)}) %collective-permute-start.7) | collective-permute-done | bytes 262176 | tf_op jit(solution)/shard_map/ppermute | solution.py:23
  109.7 4.1 %collective-permute-done.8 = bf16[2,4,128,128]{3,2,1,0:T(8,128)(2,1)S(1)} collective-permute-done((bf16[2,4,128,128]{3,2,1,0:T(8,128)(2,1)S(1)}, bf16[2,4,128,128]{3,2,1,0:T(8,128)(2,1)S(1)}, u32[]{:S(2)}, u32[]{:S(2)}) %collective-permute-start.8) | collective-permute-done | bytes 262176 | tf_op jit(solution)/shard_map/ppermute | solution.py:23
  113.9 28.2 %all_to_all.17 = bf16[8,128,128]{2,1,0:T(8,128)(2,1)S(1)} all-to-all(bf16[8,128,128]{2,1,0:T(8,128)(2,1)S(1)} %bitcast.18), channel_id=1, replica_groups=mesh['xy'=16,'c'=2,'zh'=4,'zl'=4] {'c','zh'}, dimensions={0} | all-to-all | bytes 524288 | tf_op jit(solution)/shard_map/all_to_all | solution.py:109
  142.2 0.7 copy.7
  (19 shorter events, 0.5 us)
Async XLA Ops:
  1.6 9.6 %collective-permute-start = (bf16[8,2048]{1,0:T(8,128)(2,1)S(1)}, bf16[8,2048]{1,0:T(8,128)(2,1)S(1)}, u32[]{:S(2)}, u32[]{:S(2)}) collective-permute-start(bf16[8,2048]{1,0:T(8,128)(2,1)S(1)} %get-tuple-element.17), channel_id=1, source_target_pairs={{0,16},{16,0},{1,17},{17,1},{2,18},{18,2},{3,19},{19,3},{4,20},{20... | collective-permute-start | bytes 98312 | tf_op jit(solution)/shard_map/ppermute | solution.py:126
  30.3 26.9 %copy-start = (bf16[4,4,80,512]{3,2,1,0:T(8,128)(2,1)S(1)}, bf16[4,4,80,512]{3,2,1,0:T(8,128)(2,1)}, u32[]{:S(2)}) copy-start(bf16[4,4,80,512]{3,2,1,0:T(8,128)(2,1)} %v0.1) | copy-start | bytes 3932164
  30.3 26.9 %collective-permute-start.4 = (bf16[4,4,80,512]{3,2,1,0:T(8,128)(2,1)}, bf16[4,4,80,512]{3,2,1,0:T(8,128)(2,1)}, u32[]{:S(2)}, u32[]{:S(2)}) collective-permute-start(bf16[4,4,80,512]{3,2,1,0:T(8,128)(2,1)} %v0.1), channel_id=1, source_target_pairs={{0,16},{16,0},{1,17},{17,1},{2,18},{18,2},{3,19},{19,3},{4,20},{20... | collective-permute-start | bytes 3932168 | tf_op jit(solution)/shard_map/ppermute | solution.py:134
  37.6 21.9 %collective-permute-start.5 = (bf16[4,4,80,512]{3,2,1,0:T(8,128)(2,1)S(1)}, bf16[4,4,80,512]{3,2,1,0:T(8,128)(2,1)}, u32[]{:S(2)}, u32[]{:S(2)}) collective-permute-start(bf16[4,4,80,512]{3,2,1,0:T(8,128)(2,1)S(1)} %broadcast_select_fusion.u0), channel_id=1, source_target_pairs={{0,16},{16,0},{1,17},{17,1},{2,18},{18,2},{3,19},{19,3},{4,20},{20... | collective-permute-start | bytes 3932168 | tf_op jit(solution)/shard_map/ppermute | solution.py:135
  39.5 8.4 %collective-permute-start.1 = (bf16[32,4096]{1,0:T(8,128)(2,1)S(1)}, bf16[32,4096]{1,0:T(8,128)(2,1)S(1)}, u32[]{:S(2)}, u32[]{:S(2)}) collective-permute-start(bf16[32,4096]{1,0:T(8,128)(2,1)S(1)} %all_gather.3.own), channel_id=1, source_target_pairs={{0,1},{1,2},{2,3},{3,4},{4,5},{5,6},{6,7},{7,8},{8,9},{9,10},{10,1... | collective-permute-start | bytes 786440 | tf_op jit(solution)/shard_map/ppermute | solution.py:23
  42.8 8.8 %collective-permute-start.2 = (bf16[32,4096]{1,0:T(8,128)(2,1)S(1)}, bf16[32,4096]{1,0:T(8,128)(2,1)S(1)}, u32[]{:S(2)}, u32[]{:S(2)}) collective-permute-start(bf16[32,4096]{1,0:T(8,128)(2,1)S(1)} %all_gather.3.own), channel_id=1, source_target_pairs={{0,15},{1,0},{2,1},{3,2},{4,3},{5,4},{6,5},{7,6},{8,7},{9,8},{10,9... | collective-permute-start | bytes 786440 | tf_op jit(solution)/shard_map/ppermute | solution.py:23
  44.8 12.4 %collective-permute-start.3 = (bf16[32,4096]{1,0:T(8,128)(2,1)S(1)}, bf16[32,4096]{1,0:T(8,128)(2,1)}, u32[]{:S(2)}, u32[]{:S(2)}) collective-permute-start(bf16[32,4096]{1,0:T(8,128)(2,1)S(1)} %all_gather.3.own), channel_id=1, source_target_pairs={{0,2},{1,3},{2,4},{3,5},{4,6},{5,7},{6,8},{7,9},{8,10},{9,11},{10,... | collective-permute-start | bytes 786440 | tf_op jit(solution)/shard_map/ppermute | solution.py:23
  61.4 15.6 %copy-start.2 = (f32[2048]{0:T(1024)S(1)}, f32[2048]{0:T(1024)}, u32[]{:S(2)}) copy-start(f32[2048]{0:T(1024)} %param.6) | copy-start | bytes 24580
  77.0 15.6 %copy-start.1 = (f32[8,2048]{1,0:T(8,128)}, f32[8,2048]{1,0:T(8,128)S(1)}, u32[]{:S(2)}) copy-start(f32[8,2048]{1,0:T(8,128)S(1)} %convert_reduce_fusion) | copy-start | bytes 196612
  92.6 14.4 %collective-permute-start.6 = (bf16[2,4,128,128]{3,2,1,0:T(8,128)(2,1)S(1)}, bf16[2,4,128,128]{3,2,1,0:T(8,128)(2,1)S(1)}, u32[]{:S(2)}, u32[]{:S(2)}) collective-permute-start(bf16[2,4,128,128]{3,2,1,0:T(8,128)(2,1)S(1)} %get-tuple-element.13), channel_id=1, source_target_pairs={{0,1},{1,2},{2,3},{3,4},{4,5},{5,6},{6,7},{7,8},{8,9},{9,10},{10,1... | collective-permute-start | bytes 786440 | tf_op jit(solution)/shard_map/ppermute | solution.py:23
  95.0 14.7 %collective-permute-start.7 = (bf16[2,4,128,128]{3,2,1,0:T(8,128)(2,1)S(1)}, bf16[2,4,128,128]{3,2,1,0:T(8,128)(2,1)S(1)}, u32[]{:S(2)}, u32[]{:S(2)}) collective-permute-start(bf16[2,4,128,128]{3,2,1,0:T(8,128)(2,1)S(1)} %get-tuple-element.14), channel_id=1, source_target_pairs={{0,15},{1,0},{2,1},{3,2},{4,3},{5,4},{6,5},{7,6},{8,7},{9,8},{10,9... | collective-permute-start | bytes 786440 | tf_op jit(solution)/shard_map/ppermute | solution.py:23
  97.9 15.8 %collective-permute-start.8 = (bf16[2,4,128,128]{3,2,1,0:T(8,128)(2,1)S(1)}, bf16[2,4,128,128]{3,2,1,0:T(8,128)(2,1)S(1)}, u32[]{:S(2)}, u32[]{:S(2)}) collective-permute-start(bf16[2,4,128,128]{3,2,1,0:T(8,128)(2,1)S(1)} %get-tuple-element.15), channel_id=1, source_target_pairs={{0,2},{1,3},{2,4},{3,5},{4,6},{5,7},{6,8},{7,9},{8,10},{9,11},{10,... | collective-permute-start | bytes 786440 | tf_op jit(solution)/shard_map/ppermute | solution.py:23

commit v6 on v5

--- a/solution.py
+++ b/solution.py
@@ -44,25 +44,29 @@
                 out[zh * 4 + at[1 + p], :, pl.ds(i * 512, 512)] = part[row : row + 8].astype(jnp.bfloat16)
 
 
-def adjoint_kernel(at, w, v0, v1, u0, u1, own, ahead, back, two, coeffs, blocks):
+def adjoint_kernel(at, w, v0, v1, u0, u1, coeffs, ahead, back, two):
     for k, u in enumerate((u0, u1)):
         for i in range(4):
             tall = jnp.concatenate([u[i, j] for j in range(4)], 0)
             a = lax.dot_general(tall, w[:, pl.ds(i * 512, 512)], NT, preferred_element_type=jnp.float32)
             for j in range(4):
                 coeffs[k, j, pl.ds(i * 80, 80), :] = a[j * 80 : j * 80 + 80].astype(jnp.bfloat16)
+    for place, block in ((at[4], two), (at[3], ahead), (at[2], back)):
+        place_blocks(at[0], place, coeffs, v0, v1, block)
+
+
+def own_kernel(at, coeffs, v0, v1, own):
+    place_blocks(at[0], at[1], coeffs, v0, v1, own)
+
+
+def place_blocks(core, place, coeffs, v0, v1, block):
+    cols = pl.ds(pl.multiple_of(place * 128, 128), 128)
     for k, v in enumerate((v0, v1)):
-        side = jnp.bitwise_xor(at[0], k)
+        side = jnp.bitwise_xor(core, k)
         for j in range(4):
-            tall = jnp.concatenate([v[i, j] for i in range(4)], 0)
-            block = lax.dot_general(coeffs[k, j], tall, TN, preferred_element_type=jnp.float32)
-            block = block.astype(jnp.bfloat16)
-            for q in range(4):
-                blocks[q, side, j] = block[:, q * 128 : q * 128 + 128]
-    own[...] = blocks[at[1]]
-    back[...] = blocks[at[2]]
-    ahead[...] = blocks[at[3]]
-    two[...] = blocks[at[4]]
+            tall = jnp.concatenate([v[i, j, :, cols] for i in range(4)], 0)
+            part = lax.dot_general(coeffs[k, j], tall, TN, preferred_element_type=jnp.float32)
+            block[side, j] = part.astype(jnp.bfloat16)
 
 
 SMEM = pl.BlockSpec(memory_space=pltpu.SMEM)
@@ -91,18 +95,23 @@
 
 def adjoint_part(at, weighted, v, u):
     blocks = jax.ShapeDtypeStruct((2, 4, 128, 128), jnp.bfloat16)
-    return pl.pallas_call(
+    coeffs, ahead, back, two = pl.pallas_call(
         adjoint_kernel,
-        out_shape=(blocks,) * 4,
+        out_shape=(jax.ShapeDtypeStruct((2, 4, 320, 128), jnp.bfloat16),) + (blocks,) * 3,
         in_specs=[SMEM] + [VMEM] * 5,
         out_specs=(VMEM,) * 4,
-        scratch_shapes=[
-            pltpu.VMEM((2, 4, 320, 128), jnp.bfloat16),
-            pltpu.VMEM((4, 2, 4, 128, 128), jnp.bfloat16),
-        ],
         compiler_params=ROOM,
         name="adjoint_part",
     )(at, weighted, *v, *u)
+    own = pl.pallas_call(
+        own_kernel,
+        out_shape=blocks,
+        in_specs=[SMEM] + [VMEM] * 3,
+        out_specs=VMEM,
+        compiler_params=ROOM,
+        name="own_part",
+    )(at, coeffs, *v)
+    return own, ahead, back, two
 
 
 def exchange(blocks, axes):
@@ -129,8 +138,8 @@
     two = turned(far, 2)
     ahead = turned(far, 1)
     back = turned(far, -1)
-    levels = lax.broadcasted_iota(jnp.int32, (1, 1, 80, 1), 2)
-    ranked = jnp.where(levels < tile_ranks[:, :, None, None], u_factors, jnp.zeros_like(u_factors))
+    kept_ranks = lax.broadcasted_iota(jnp.int32, (4, 4, 80), 2) < tile_ranks[:, :, None]
+    ranked = jnp.where(kept_ranks[..., None], u_factors, jnp.zeros_like(u_factors))
     v = (v_factors, swap(v_factors))
     u = (ranked, swap(ranked))
     part = forward_part(at, (far, ahead, back, two), v, u)

time: 144 us -> 142 us (0.986)
  blocking collectives: 75.1 us -> 79.6 us
  starting transfers between devices: 39.1 us -> 34.7 us
  waiting for transfers between devices: 16 us -> 12.7 us
  Pallas kernels: 7.43 us -> 9.24 us
    all_to_all x3, blocking collectives: 56 us -> 60.4 us  [exchange(): return lax.all_to_all(blocks, axes, split_axis=0, concat_axis=0, tiled=True)]
    ppermute x6, starting transfers between devices: 22.7 us -> 18.3 us  [turned(): return lax.ppermute(x, PAIR_LINE, pairs)]
    ppermute x6, waiting for transfers between devices: 16 us -> 12.6 us  [turned(): return lax.ppermute(x, PAIR_LINE, pairs)]
    pallas_call x1 -> x2, Pallas kernels: 3.25 us -> 5.06 us  [the longest x1 3.33 us: adjoint_part(): pl.pallas_call(adjoint_kernel, out_shape=(jax.ShapeDtypeStruct((2, 4, 320...]
  transfers between devices with their start and end apart: 9 -> 9, of which waited for: 5 -> 6; matrix products, arithmetic and copies ran while one was open for 2% -> 2% of each run, Pallas kernels for 2% -> 3%
where the time goes in v6:
time: 142 us; the launch traced here: 141 us
  blocking collectives  79.6 us (56%)
  starting transfers between devices  34.7 us (24%)
  waiting for transfers between devices  12.7 us (9%)
  Pallas kernels  9.24 us (7%)
  other arithmetic  3.49 us (2%)
    all_to_all x3, blocking collectives, exchange(): return lax.all_to_all(blocks, axes, split_axis=0, concat_axis=0, tiled=True)  60.4 us
    all_gather x1, blocking collectives, both_products(): far = lax.all_gather(block, 'zh', axis=0, tiled=True)  19.2 us
    ppermute x6, starting transfers between devices, turned(): return lax.ppermute(x, PAIR_LINE, pairs)  18.3 us
    ppermute x6, waiting for transfers between devices, turned(): return lax.ppermute(x, PAIR_LINE, pairs)  12.6 us
    ppermute x1, starting transfers between devices, both_products(): block = jnp.concatenate([kept, swap(given)], 1)  8.75 us
    ppermute x1, starting transfers between devices, both_products(): v = (v_factors, swap(v_factors))  5.74 us
    pallas_call x1, Pallas kernels, adjoint_part(): pl.pallas_call(adjoint_kernel, out_shape=(jax.ShapeDtypeStruct((2, 4, 320...  3.33 us
  transfers between devices with their start and end apart: 9, of which 6 were waited for; matrix products, arithmetic and copies ran while one was open for 2% of the time, Pallas kernels for 3%

profile of v6, /device:TPU:1, one launch (start us, length us, event | category | flops | bytes accessed | tf_op | source)
XLA Modules:
  0.0 141.3 jit_solution(1932547721498033957)
XLA Ops:
  0.6 0.9 convert_bitcast_fusion
  1.6 8.7 %collective-permute-start = (bf16[8,2048]{1,0:T(8,128)(2,1)S(1)}, bf16[8,2048]{1,0:T(8,128)(2,1)S(1)}, u32[]{:S(2)}, u32[]{:S(2)}) collective-permute-start(bf16[8,2048]{1,0:T(8,128)(2,1)S(1)} %get-tuple-element.17), channel_id=1, source_target_pairs={{0,16},{16,0},{1,17},{17,1},{2,18},{18,2},{3,19},{19,3},{4,20},{20... | collective-permute-start | bytes 98312 | tf_op jit(solution)/shard_map/ppermute | solution.py:135
  10.3 0.8 iota_compare_fusion
  11.2 19.2 %all_gather.3.own = bf16[32,4096]{1,0:T(8,128)(2,1)S(1)} all-gather(bf16[8,4096]{1,0:T(8,128)(2,1)S(1)} %pad_maximum_fusion), channel_id=1, replica_groups=mesh['xy'=16,'c'=2,'zh'=4,'zl'=4] {'zh'}, dimensions={0}, use_global_device_ids=true | all-gather | bytes 327680 | tf_op jit(solution)/shard_map/all_gather | solution.py:136
  30.3 5.7 %collective-permute-start.4 = (bf16[4,4,80,512]{3,2,1,0:T(8,128)(2,1)}, bf16[4,4,80,512]{3,2,1,0:T(8,128)(2,1)}, u32[]{:S(2)}, u32[]{:S(2)}) collective-permute-start(bf16[4,4,80,512]{3,2,1,0:T(8,128)(2,1)} %v0.2), channel_id=1, source_target_pairs={{0,16},{16,0},{1,17},{17,1},{2,18},{18,2},{3,19},{19,3},{4,20},{20... | collective-permute-start | bytes 3932168 | tf_op jit(solution)/shard_map/ppermute | solution.py:143
  36.1 1.6 %broadcast_select_fusion.u0 = bf16[4,4,80,512]{3,2,1,0:T(8,128)(2,1)S(1)} fusion(bf16[4,4,80,512]{3,2,1,0:T(8,128)(2,1)} %param.8, pred[4,4,80]{2,1,0:T(4,128)(4,1)S(1)} %iota_compare_fusion), kind=kLoop, calls=%fused_computation | loop fusion | flops 655360 | bytes 2622720 | tf_op jit(solution)/shard_map/jit(_where)/select_n | solution.py:142
  37.6 1.9 %collective-permute-start.5 = (bf16[4,4,80,512]{3,2,1,0:T(8,128)(2,1)S(1)}, bf16[4,4,80,512]{3,2,1,0:T(8,128)(2,1)}, u32[]{:S(2)}, u32[]{:S(2)}) collective-permute-start(bf16[4,4,80,512]{3,2,1,0:T(8,128)(2,1)S(1)} %broadcast_select_fusion.u0), channel_id=1, source_target_pairs={{0,16},{16,0},{1,17},{17,1},{2,18},{18,2},{3,19},{19,3},{4,20},{20... | collective-permute-start | bytes 3932168 | tf_op jit(solution)/shard_map/ppermute | solution.py:144
  39.5 2.6 %collective-permute-start.3 = (bf16[32,4096]{1,0:T(8,128)(2,1)S(1)}, bf16[32,4096]{1,0:T(8,128)(2,1)S(1)}, u32[]{:S(2)}, u32[]{:S(2)}) collective-permute-start(bf16[32,4096]{1,0:T(8,128)(2,1)S(1)} %all_gather.3.own), channel_id=1, source_target_pairs={{0,2},{1,3},{2,4},{3,5},{4,6},{5,7},{6,8},{7,9},{8,10},{9,11},{10,... | collective-permute-start | bytes 786440 | tf_op jit(solution)/shard_map/ppermute | solution.py:23
  42.2 3.7 %collective-permute-start.2 = (bf16[32,4096]{1,0:T(8,128)(2,1)S(1)}, bf16[32,4096]{1,0:T(8,128)(2,1)S(1)}, u32[]{:S(2)}, u32[]{:S(2)}) collective-permute-start(bf16[32,4096]{1,0:T(8,128)(2,1)S(1)} %all_gather.3.own), channel_id=1, source_target_pairs={{0,15},{1,0},{2,1},{3,2},{4,3},{5,4},{6,5},{7,6},{8,7},{9,8},{10,9... | collective-permute-start | bytes 786440 | tf_op jit(solution)/shard_map/ppermute | solution.py:23
  45.9 2.8 %collective-permute-start.1 = (bf16[32,4096]{1,0:T(8,128)(2,1)S(1)}, bf16[32,4096]{1,0:T(8,128)(2,1)}, u32[]{:S(2)}, u32[]{:S(2)}) collective-permute-start(bf16[32,4096]{1,0:T(8,128)(2,1)S(1)} %all_gather.3.own), channel_id=1, source_target_pairs={{0,1},{1,2},{2,3},{3,4},{4,5},{5,6},{6,7},{7,8},{8,9},{9,10},{10,1... | collective-permute-start | bytes 786440 | tf_op jit(solution)/shard_map/ppermute | solution.py:23
  48.8 3.7 %collective-permute-done.3.two = bf16[32,4096]{1,0:T(8,128)(2,1)S(1)} collective-permute-done((bf16[32,4096]{1,0:T(8,128)(2,1)S(1)}, bf16[32,4096]{1,0:T(8,128)(2,1)S(1)}, u32[]{:S(2)}, u32[]{:S(2)}) %collective-permute-start.3) | collective-permute-done | bytes 262176 | tf_op jit(solution)/shard_map/ppermute | solution.py:23
  52.5 3.5 %collective-permute-done.2.back = bf16[32,4096]{1,0:T(8,128)(2,1)S(1)} collective-permute-done((bf16[32,4096]{1,0:T(8,128)(2,1)S(1)}, bf16[32,4096]{1,0:T(8,128)(2,1)S(1)}, u32[]{:S(2)}, u32[]{:S(2)}) %collective-permute-start.2) | collective-permute-done | bytes 262176 | tf_op jit(solution)/shard_map/ppermute | solution.py:23
  56.4 2.2 %forward_coeffs.1.coeffs = bf16[4,640,128]{2,1,0:T(8,128)(2,1)S(1)} custom-call(bf16[32,4096]{1,0:T(8,128)(2,1)S(1)} %all_gather.3.own, bf16[32,4096]{1,0:T(8,128)(2,1)} %collective-permute-done.1.ahead, bf16[32,4096]{1,0:T(8,128)(2,1)S(1)} %collective-permute-done.2.back, bf16[32,4096]{1,0:T(8,128)(2,1)S(1)} %collective-permute-done.3.two, ...), custom_call_target="tpu_custom_call" | custom-call | tf_op jit(solution)/shard_map/forward_coeffs/pallas_call | solution.py:78
  58.7 1.9 %forward_part.1 = bf16[16,8,2048]{2,1,0:T(8,128)(2,1)S(1)} custom-call(s32[5]{0:T(128)S(1)} %stack.23.at, bf16[4,640,128]{2,1,0:T(8,128)(2,1)S(1)} %forward_coeffs.1.coeffs, bf16[4,4,80,512]{3,2,1,0:T(8,128)(2,1)S(1)} %broadcast_select_fusion.u0, bf16[4,4,80,512]{3,2,1,0:T(8,128)(2,1)} %collective-permute-done.5.u1), custom_call_target="tpu_custom_call" | custom-call | tf_op jit(solution)/shard_map/forward_part/pallas_call | solution.py:86
  60.7 15.8 %all_to_all.15 = bf16[16,8,2048]{2,1,0:T(8,128)(2,1)S(1)} all-to-all(bf16[16,8,2048]{2,1,0:T(8,128)(2,1)S(1)} %forward_part.1), channel_id=1, replica_groups=mesh['xy'=16,'c'=2,'zh'=4,'zl'=4] {'xy'}, dimensions={0} | all-to-all | bytes 1048576 | tf_op jit(solution)/shard_map/all_to_all | solution.py:118
  76.7 11.9 %all_to_all.16 = bf16[16,8,2048]{2,1,0:T(8,128)(2,1)S(1)} all-to-all(bf16[16,8,2048]{2,1,0:T(8,128)(2,1)S(1)} %broadcast_in_dim.19), channel_id=1, replica_groups=mesh['xy'=16,'c'=2,'zh'=4,'zl'=4] {'xy'}, dimensions={0} | all-to-all | bytes 1048576 | tf_op jit(solution)/shard_map/all_to_all | solution.py:118
  88.5 3.3 %adjoint_part.1 = (bf16[2,4,320,128]{3,2,1,0:T(8,128)(2,1)S(1)}, bf16[2,4,128,128]{3,2,1,0:T(8,128)(2,1)S(1)}, bf16[2,4,128,128]{3,2,1,0:T(8,128)(2,1)S(1)}, bf16[2,4,128,128]{3,2,1,0:T(8,128)(2,1)S(1)}) custom-call(s32[5]{0:T(128)S(1)} %stack.23.at, bf16[128,2048]{1,0:T(8,128)(2,1)S(1)} %bitcast.17, bf16[4,4,80,512]{3,2,1,0:T(8,128)(2,1)S(1)} %copy-done, ...), custom_call_target="tpu_custom_call" | custom-call | tf_op jit(solution)/shard_map/adjoint_part/pallas_call | solution.py:98
  91.9 2.7 %collective-permute-start.6 = (bf16[2,4,128,128]{3,2,1,0:T(8,128)(2,1)S(1)}, bf16[2,4,128,128]{3,2,1,0:T(8,128)(2,1)S(1)}, u32[]{:S(2)}, u32[]{:S(2)}) collective-permute-start(bf16[2,4,128,128]{3,2,1,0:T(8,128)(2,1)S(1)} %get-tuple-element.13), channel_id=1, source_target_pairs={{0,1},{1,2},{2,3},{3,4},{4,5},{5,6},{6,7},{7,8},{8,9},{9,10},{10,1... | collective-permute-start | bytes 786440 | tf_op jit(solution)/shard_map/ppermute | solution.py:23
  94.6 2.6 %collective-permute-start.7 = (bf16[2,4,128,128]{3,2,1,0:T(8,128)(2,1)S(1)}, bf16[2,4,128,128]{3,2,1,0:T(8,128)(2,1)S(1)}, u32[]{:S(2)}, u32[]{:S(2)}) collective-permute-start(bf16[2,4,128,128]{3,2,1,0:T(8,128)(2,1)S(1)} %get-tuple-element.14), channel_id=1, source_target_pairs={{0,15},{1,0},{2,1},{3,2},{4,3},{5,4},{6,5},{7,6},{8,7},{9,8},{10,9... | collective-permute-start | bytes 786440 | tf_op jit(solution)/shard_map/ppermute | solution.py:23
  97.2 3.8 %collective-permute-start.8 = (bf16[2,4,128,128]{3,2,1,0:T(8,128)(2,1)S(1)}, bf16[2,4,128,128]{3,2,1,0:T(8,128)(2,1)S(1)}, u32[]{:S(2)}, u32[]{:S(2)}) collective-permute-start(bf16[2,4,128,128]{3,2,1,0:T(8,128)(2,1)S(1)} %get-tuple-element.15), channel_id=1, source_target_pairs={{0,2},{1,3},{2,4},{3,5},{4,6},{5,7},{6,8},{7,9},{8,10},{9,11},{10,... | collective-permute-start | bytes 786440 | tf_op jit(solution)/shard_map/ppermute | solution.py:23
  101.0 1.7 %own_part.1 = bf16[2,4,128,128]{3,2,1,0:T(8,128)(2,1)S(1)} custom-call(s32[5]{0:T(128)S(1)} %stack.23.at, bf16[2,4,320,128]{3,2,1,0:T(8,128)(2,1)S(1)} %get-tuple-element.12.coeffs, bf16[4,4,80,512]{3,2,1,0:T(8,128)(2,1)S(1)} %copy-done, bf16[4,4,80,512]{3,2,1,0:T(8,128)(2,1)} %collective-permute-done.4.v1), custom_call_target="tpu_custom_call" | custom-call | tf_op jit(solution)/shard_map/own_part/pallas_call | solution.py:106
  102.8 0.8 collective-permute-done.7
  103.5 4.2 %collective-permute-done.8 = bf16[2,4,128,128]{3,2,1,0:T(8,128)(2,1)S(1)} collective-permute-done((bf16[2,4,128,128]{3,2,1,0:T(8,128)(2,1)S(1)}, bf16[2,4,128,128]{3,2,1,0:T(8,128)(2,1)S(1)}, u32[]{:S(2)}, u32[]{:S(2)}) %collective-permute-start.8) | collective-permute-done | bytes 262176 | tf_op jit(solution)/shard_map/ppermute | solution.py:23
  107.9 32.7 %all_to_all.17 = bf16[8,128,128]{2,1,0:T(8,128)(2,1)S(1)} all-to-all(bf16[8,128,128]{2,1,0:T(8,128)(2,1)S(1)} %bitcast.18), channel_id=1, replica_groups=mesh['xy'=16,'c'=2,'zh'=4,'zl'=4] {'c','zh'}, dimensions={0} | all-to-all | bytes 524288 | tf_op jit(solution)/shard_map/all_to_all | solution.py:118
  (20 shorter events, 1.6 us)
Async XLA Ops:
  1.6 9.6 %collective-permute-start = (bf16[8,2048]{1,0:T(8,128)(2,1)S(1)}, bf16[8,2048]{1,0:T(8,128)(2,1)S(1)}, u32[]{:S(2)}, u32[]{:S(2)}) collective-permute-start(bf16[8,2048]{1,0:T(8,128)(2,1)S(1)} %get-tuple-element.17), channel_id=1, source_target_pairs={{0,16},{16,0},{1,17},{17,1},{2,18},{18,2},{3,19},{19,3},{4,20},{20... | collective-permute-start | bytes 98312 | tf_op jit(solution)/shard_map/ppermute | solution.py:135
  30.3 26.1 %copy-start = (bf16[4,4,80,512]{3,2,1,0:T(8,128)(2,1)S(1)}, bf16[4,4,80,512]{3,2,1,0:T(8,128)(2,1)}, u32[]{:S(2)}) copy-start(bf16[4,4,80,512]{3,2,1,0:T(8,128)(2,1)} %v0.2) | copy-start | bytes 3932164
  30.3 26.1 %collective-permute-start.4 = (bf16[4,4,80,512]{3,2,1,0:T(8,128)(2,1)}, bf16[4,4,80,512]{3,2,1,0:T(8,128)(2,1)}, u32[]{:S(2)}, u32[]{:S(2)}) collective-permute-start(bf16[4,4,80,512]{3,2,1,0:T(8,128)(2,1)} %v0.2), channel_id=1, source_target_pairs={{0,16},{16,0},{1,17},{17,1},{2,18},{18,2},{3,19},{19,3},{4,20},{20... | collective-permute-start | bytes 3932168 | tf_op jit(solution)/shard_map/ppermute | solution.py:143
  37.6 21.1 %collective-permute-start.5 = (bf16[4,4,80,512]{3,2,1,0:T(8,128)(2,1)S(1)}, bf16[4,4,80,512]{3,2,1,0:T(8,128)(2,1)}, u32[]{:S(2)}, u32[]{:S(2)}) collective-permute-start(bf16[4,4,80,512]{3,2,1,0:T(8,128)(2,1)S(1)} %broadcast_select_fusion.u0), channel_id=1, source_target_pairs={{0,16},{16,0},{1,17},{17,1},{2,18},{18,2},{3,19},{19,3},{4,20},{20... | collective-permute-start | bytes 3932168 | tf_op jit(solution)/shard_map/ppermute | solution.py:144
  39.5 13.0 %collective-permute-start.3 = (bf16[32,4096]{1,0:T(8,128)(2,1)S(1)}, bf16[32,4096]{1,0:T(8,128)(2,1)S(1)}, u32[]{:S(2)}, u32[]{:S(2)}) collective-permute-start(bf16[32,4096]{1,0:T(8,128)(2,1)S(1)} %all_gather.3.own), channel_id=1, source_target_pairs={{0,2},{1,3},{2,4},{3,5},{4,6},{5,7},{6,8},{7,9},{8,10},{9,11},{10,... | collective-permute-start | bytes 786440 | tf_op jit(solution)/shard_map/ppermute | solution.py:23
  42.2 13.9 %collective-permute-start.2 = (bf16[32,4096]{1,0:T(8,128)(2,1)S(1)}, bf16[32,4096]{1,0:T(8,128)(2,1)S(1)}, u32[]{:S(2)}, u32[]{:S(2)}) collective-permute-start(bf16[32,4096]{1,0:T(8,128)(2,1)S(1)} %all_gather.3.own), channel_id=1, source_target_pairs={{0,15},{1,0},{2,1},{3,2},{4,3},{5,4},{6,5},{7,6},{8,7},{9,8},{10,9... | collective-permute-start | bytes 786440 | tf_op jit(solution)/shard_map/ppermute | solution.py:23
  45.9 10.5 %collective-permute-start.1 = (bf16[32,4096]{1,0:T(8,128)(2,1)S(1)}, bf16[32,4096]{1,0:T(8,128)(2,1)}, u32[]{:S(2)}, u32[]{:S(2)}) collective-permute-start(bf16[32,4096]{1,0:T(8,128)(2,1)S(1)} %all_gather.3.own), channel_id=1, source_target_pairs={{0,1},{1,2},{2,3},{3,4},{4,5},{5,6},{6,7},{7,8},{8,9},{9,10},{10,1... | collective-permute-start | bytes 786440 | tf_op jit(solution)/shard_map/ppermute | solution.py:23
  60.6 15.9 %copy-start.2 = (f32[2048]{0:T(1024)S(1)}, f32[2048]{0:T(1024)}, u32[]{:S(2)}) copy-start(f32[2048]{0:T(1024)} %param.6) | copy-start | bytes 24580
  76.6 15.3 %copy-start.1 = (f32[8,2048]{1,0:T(8,128)}, f32[8,2048]{1,0:T(8,128)S(1)}, u32[]{:S(2)}) copy-start(f32[8,2048]{1,0:T(8,128)S(1)} %convert_reduce_fusion) | copy-start | bytes 196612
  91.9 10.9 %collective-permute-start.6 = (bf16[2,4,128,128]{3,2,1,0:T(8,128)(2,1)S(1)}, bf16[2,4,128,128]{3,2,1,0:T(8,128)(2,1)S(1)}, u32[]{:S(2)}, u32[]{:S(2)}) collective-permute-start(bf16[2,4,128,128]{3,2,1,0:T(8,128)(2,1)S(1)} %get-tuple-element.13), channel_id=1, source_target_pairs={{0,1},{1,2},{2,3},{3,4},{4,5},{5,6},{6,7},{7,8},{8,9},{9,10},{10,1... | collective-permute-start | bytes 786440 | tf_op jit(solution)/shard_map/ppermute | solution.py:23
  94.6 8.9 %collective-permute-start.7 = (bf16[2,4,128,128]{3,2,1,0:T(8,128)(2,1)S(1)}, bf16[2,4,128,128]{3,2,1,0:T(8,128)(2,1)S(1)}, u32[]{:S(2)}, u32[]{:S(2)}) collective-permute-start(bf16[2,4,128,128]{3,2,1,0:T(8,128)(2,1)S(1)} %get-tuple-element.14), channel_id=1, source_target_pairs={{0,15},{1,0},{2,1},{3,2},{4,3},{5,4},{6,5},{7,6},{8,7},{9,8},{10,9... | collective-permute-start | bytes 786440 | tf_op jit(solution)/shard_map/ppermute | solution.py:23
  97.2 10.6 %collective-permute-start.8 = (bf16[2,4,128,128]{3,2,1,0:T(8,128)(2,1)S(1)}, bf16[2,4,128,128]{3,2,1,0:T(8,128)(2,1)S(1)}, u32[]{:S(2)}, u32[]{:S(2)}) collective-permute-start(bf16[2,4,128,128]{3,2,1,0:T(8,128)(2,1)S(1)} %get-tuple-element.15), channel_id=1, source_target_pairs={{0,2},{1,3},{2,4},{3,5},{4,6},{5,7},{6,8},{7,9},{8,10},{9,11},{10,... | collective-permute-start | bytes 786440 | tf_op jit(solution)/shard_map/ppermute | solution.py:23
